TPU v7x, 32 devices: a whole 2x2x4 slice. The times are simulated.
32 devices in a mesh: fsdp: 16 (over z, y, x), mat: 2 (over core).
Axes of the slice: x: 2, y: 2, z: 4, core: 2. Of those that a mesh axis runs over, the one named last changes fastest.
Arguments:
- momentum: float32 [8192, 4096], P(('mat', 'fsdp')), parts along dimension 0, may hold values from -6 to 6
- grad: bfloat16 [8192, 4096], P(('mat', 'fsdp')), parts along dimension 0, may hold values from -6 to 6
- q_basis: float32 [8192, 512], P(('mat', 'fsdp')), parts along dimension 0, may hold values from -6 to 6
Outputs:
- momentum_next: float32 [8192, 4096], P(('mat', 'fsdp')), parts along dimension 0
- update: bfloat16 [8192, 4096], P(('mat', 'fsdp')), parts along dimension 0
- q_next: float32 [8192, 512], P(('mat', 'fsdp')), parts along dimension 0
There are 2 independent parts, one for each index of `mat`. A program takes and returns all parts, laid end to end along the dimension named above; each array names one. Nothing has to cross between parts.
All inputs are finite; a program needn't handle non-finite values.
Results may differ from a plain program's by a relative error of at most 0.0076.
Values may be sent and summed in bfloat16 or wider, within the bound.
A program may use at most 128 MiB of HBM per device.

v0:
```python
import functools
import math

import jax
import jax.numpy as jnp
from jax import lax
from jax.experimental import pallas as pl
from jax.experimental.pallas import tpu as pltpu
from jax.sharding import PartitionSpec as P

damping = 0.95
epsilon = 1e-06
HIGHEST = lax.Precision.HIGHEST
MESH = pl.DeviceIdType.MESH


def grid_of(mesh):
    n = mesh.shape["fsdp"]
    at = list(mesh.axis_names).index("fsdp")
    try:
        line = mesh.devices.swapaxes(0, at).reshape(n, -1)[:, 0]
        spots = [tuple(d.coords) for d in line]
        axes = []
        for d in range(3):
            size = len({s[d] for s in spots})
            if size > 1:
                stride = next(i for i in range(n) if spots[i][d] != spots[0][d])
                axes.append((stride, size))
        sizes = [size for _, size in sorted(axes, reverse=True)]
        if math.prod(sizes) == n:
            return tuple([1] * (3 - len(sizes)) + sizes)
    except AttributeError:
        pass
    return (n // 4, 2, 2) if n % 4 == 0 else (1, 1, n)


def cut(rows, unit, sizes):
    units = rows // unit
    long_axis = max(range(3), key=lambda d: sizes[d])
    first, second = [d for d in range(3) if d != long_axis]
    tail = units // 8
    pairs = 2 if units >= 8 else 1
    share, extra = divmod(units - tail, 2 * pairs)
    plan = [(tail, (first, second, long_axis), 0)]
    for k in range(2 * pairs):
        short = (first, second) if k % 2 == 0 else (second, first)
        plan.append((share + (k < extra), (long_axis,) + short, k // 2))
    pieces, start = [], 0
    for count, order, wave in plan:
        if count:
            pieces.append((start, count * unit, order, wave))
        start += count * unit
    return pieces


def wavefront(pieces, phases):
    steps = [(piece[3] + phase, phase, p) for p, piece in enumerate(pieces) for phase in range(phases)]
    return [(phase, p) for _, phase, p in sorted(steps)]


def position(sizes):
    me = lax.axis_index("fsdp")
    return [
        lax.div(me, sizes[1] * sizes[2]),
        lax.rem(lax.div(me, sizes[2]), sizes[1]),
        lax.rem(me, sizes[2]),
    ]


def shifted(mine, sizes, d, off):
    return lax.rem(mine[d] + off, sizes[d])


def device_at(mine, sizes, d, coordinate):
    spot = list(mine)
    spot[d] = coordinate
    return {"fsdp": (spot[0] * sizes[1] + spot[1]) * sizes[2] + spot[2]}


def greet(mine, sizes):
    barrier = pltpu.get_barrier_semaphore()
    for d in range(3):
        for off in range(1, sizes[d]):
            target = device_at(mine, sizes, d, shifted(mine, sizes, d, off))
            pl.semaphore_signal(barrier, inc=1, device_id=target, device_id_type=MESH)
    pl.semaphore_wait(barrier, sum(sizes) - 3)


def gather_kernel(sizes, pieces, x_ref, o_ref, own_sem, send_sem, recv_sem):
    mine = position(sizes)
    own = pltpu.make_async_copy(x_ref, o_ref.at[mine[0], mine[1], mine[2]], own_sem)
    own.start()
    greet(mine, sizes)

    def block(piece, phase, coordinate):
        start, rows, order, _ = piece
        index = list(mine)
        index[order[phase]] = coordinate
        for d in order[:phase]:
            index[d] = slice(None)
        return o_ref.at[index[0], index[1], index[2], pl.ds(start, rows)]

    sent = []
    own_here = False
    for phase, p in wavefront(pieces, 3):
        piece = pieces[p]
        if phase:
            if not own_here:
                own.wait()
                own_here = True
            d = piece[2][phase - 1]
            for off in range(1, sizes[d]):
                landed = block(piece, phase - 1, shifted(mine, sizes, d, sizes[d] - off))
                pltpu.make_async_copy(landed, landed, recv_sem.at[p, phase - 1, off]).wait()
        d = piece[2][phase]
        for off in range(1, sizes[d]):
            target = block(piece, phase, mine[d])
            source = x_ref.at[pl.ds(piece[0], piece[1])] if phase == 0 else target
            copy = pltpu.make_async_remote_copy(
                src_ref=source,
                dst_ref=target,
                send_sem=send_sem.at[p, phase, off],
                recv_sem=recv_sem.at[p, phase, off],
                device_id=device_at(mine, sizes, d, shifted(mine, sizes, d, off)),
                device_id_type=MESH,
            )
            copy.start()
            sent.append(copy)
    for p, piece in enumerate(pieces):
        d = piece[2][2]
        for off in range(1, sizes[d]):
            landed = block(piece, 2, shifted(mine, sizes, d, sizes[d] - off))
            pltpu.make_async_copy(landed, landed, recv_sem.at[p, 2, off]).wait()
    for copy in sent:
        copy.wait_send()


def gather(x, sizes, number):
    rows, columns = x.shape
    unit = 8 if x.dtype == jnp.float32 else 16
    pieces = cut(rows, unit, sizes)
    sems = pltpu.SemaphoreType.DMA((len(pieces), 3, max(sizes)))
    out = pl.pallas_call(
        functools.partial(gather_kernel, sizes, pieces),
        out_shape=jax.ShapeDtypeStruct(sizes + (rows, columns), x.dtype),
        in_specs=[pl.BlockSpec(memory_space=pltpu.VMEM)],
        out_specs=pl.BlockSpec(memory_space=pltpu.VMEM),
        scratch_shapes=[pltpu.SemaphoreType.DMA, sems, sems],
        compiler_params=pltpu.CompilerParams(
            collective_id=number, has_side_effects=True, vmem_limit_bytes=32 * 2**20
        ),
        name=f"gather_{number}",
    )(x)
    return out.reshape(math.prod(sizes) * rows, columns)


def reduce_kernel(sizes, pieces, x_ref, o_ref, *scratch):
    mine = position(sizes)
    count = len(pieces)
    landing = scratch[: 3 * count]
    sums = scratch[3 * count : 5 * count]
    send_sem, recv_sem = scratch[5 * count :]
    greet(mine, sizes)
    sent = []

    def send(p, phase, d, off, source):
        copy = pltpu.make_async_remote_copy(
            src_ref=source,
            dst_ref=landing[3 * p + phase].at[off - 1],
            send_sem=send_sem.at[p, phase, off],
            recv_sem=recv_sem.at[p, phase, off],
            device_id=device_at(mine, sizes, d, shifted(mine, sizes, d, off)),
            device_id_type=MESH,
        )
        copy.start()
        sent.append(copy)

    def arrive(p, phase, d):
        for off in range(1, sizes[d]):
            here = landing[3 * p + phase].at[off - 1]
            pltpu.make_async_copy(here, here, recv_sem.at[p, phase, off]).wait()

    def begin(p, start, rows, order):
        d = order[2]
        for off in range(1, sizes[d]):
            index = [slice(None)] * 3
            index[d] = shifted(mine, sizes, d, off)
            send(p, 0, d, off, x_ref.at[index[0], index[1], index[2], pl.ds(start, rows)])

    def first_sums(p, start, rows, order):
        a, b, c = order
        arrive(p, 0, c)
        low, high = min(a, b), max(a, b)
        for off in list(range(1, sizes[b])) + [0]:
            at_b = shifted(mine, sizes, b, off)

            def one(at_a, _, off=off, at_b=at_b):
                index = [None] * 3
                index[a], index[b], index[c] = at_a, at_b, mine[c]
                total = x_ref[index[0], index[1], index[2], pl.ds(start, rows)].astype(jnp.float32)
                for k in range(sizes[c] - 1):
                    total += landing[3 * p][k, index[low], index[high]].astype(jnp.float32)
                if off:
                    sums[2 * p][off - 1, at_a] = total.astype(x_ref.dtype)
                else:
                    sums[2 * p + 1][at_a] = total
                return 0

            lax.fori_loop(0, sizes[a], one, 0)
        for off in range(1, sizes[b]):
            send(p, 1, b, off, sums[2 * p].at[off - 1])

    def second_sums(p, start, rows, order):
        a, b, c = order
        arrive(p, 1, b)
        for off in list(range(1, sizes[a])) + [0]:
            at_a = shifted(mine, sizes, a, off)
            total = sums[2 * p + 1][at_a]
            for k in range(sizes[b] - 1):
                total += landing[3 * p + 1][k, at_a].astype(jnp.float32)
            if off:
                landing[3 * p + 2][sizes[a] - 1 + off - 1] = total.astype(x_ref.dtype)
            else:
                sums[2 * p + 1][at_a] = total
        for off in range(1, sizes[a]):
            send(p, 2, a, off, landing[3 * p + 2].at[sizes[a] - 1 + off - 1])

    def last_sums(p, start, rows, order):
        a = order[0]
        arrive(p, 2, a)
        total = sums[2 * p + 1][mine[a]]
        for k in range(sizes[a] - 1):
            total += landing[3 * p + 2][k].astype(jnp.float32)
        o_ref[pl.ds(start, rows)] = total

    stages = (begin, first_sums, second_sums, last_sums)
    for phase, p in wavefront(pieces, 4):
        stages[phase](p, *pieces[p][:3])
    for copy in sent:
        copy.wait_send()


def reduce_scatter(x, sizes, number):
    n = math.prod(sizes)
    rows, columns = x.shape[0] // n, x.shape[1]
    unit = 8 if x.dtype == jnp.float32 else 16
    pieces = cut(rows, unit, sizes)
    landing, sums = [], []
    for _, part, (a, b, c), _ in pieces:
        low, high = min(a, b), max(a, b)
        many = lambda k: max(k, 1)
        landing += [
            pltpu.VMEM((many(sizes[c] - 1), sizes[low], sizes[high], part, columns), x.dtype),
            pltpu.VMEM((many(sizes[b] - 1), sizes[a], part, columns), x.dtype),
            pltpu.VMEM((many(2 * (sizes[a] - 1)), part, columns), x.dtype),
        ]
        sums += [
            pltpu.VMEM((many(sizes[b] - 1), sizes[a], part, columns), x.dtype),
            pltpu.VMEM((sizes[a], part, columns), jnp.float32),
        ]
    sems = pltpu.SemaphoreType.DMA((len(pieces), 3, max(sizes)))
    return pl.pallas_call(
        functools.partial(reduce_kernel, sizes, pieces),
        out_shape=jax.ShapeDtypeStruct((rows, columns), jnp.float32),
        in_specs=[pl.BlockSpec(memory_space=pltpu.VMEM)],
        out_specs=pl.BlockSpec(memory_space=pltpu.VMEM),
        scratch_shapes=landing + sums + [sems, sems],
        compiler_params=pltpu.CompilerParams(
            collective_id=number, has_side_effects=True, vmem_limit_bytes=40 * 2**20
        ),
        name=f"reduce_{number}",
    )(x.reshape(sizes + (rows, columns)))


def dot_first(left, right):
    return lax.dot_general(
        left, right, (((0,), (0,)), ((), ())), precision=HIGHEST, preferred_element_type=jnp.float32
    )


def three(x):
    high = x.astype(jnp.bfloat16).astype(jnp.float32)
    rest = x - high
    middle = rest.astype(jnp.bfloat16).astype(jnp.float32)
    return high, middle, rest - middle


def short_dot(left, right):
    h, m, l = three(left)
    lefts = jnp.concatenate([h, h, m, m, h, l], axis=0).astype(jnp.bfloat16)
    h, m, l = three(right)
    rights = jnp.concatenate([h, m, h, m, l, h], axis=0).astype(jnp.bfloat16)
    return lax.dot_general(
        lefts, rights, (((0,), (0,)), ((), ())), preferred_element_type=jnp.float32
    )


def inverse_kernel(size, width, g_ref, x_ref, a_ref, d_ref):
    eye = lax.broadcasted_iota(jnp.int32, (size, size), 0) == lax.broadcasted_iota(
        jnp.int32, (size, size), 1
    )
    gram = g_ref[...]
    trace = jnp.sum(jnp.where(eye, gram, 0.0), keepdims=True)
    a_ref[...] = gram + jnp.where(eye, 0.0001 * trace / size, 0.0)
    x_ref[...] = jnp.where(eye, 1.0, 0.0)
    strip = lax.broadcasted_iota(jnp.int32, (8, width), 0)
    lane = lax.broadcasted_iota(jnp.int32, (8, width), 1)
    small_eye = jnp.where(
        lax.broadcasted_iota(jnp.int32, (width, width), 0)
        == lax.broadcasted_iota(jnp.int32, (width, width), 1),
        1.0,
        0.0,
    )

    def group(g, _):
        first = pl.multiple_of(g * 8, 8)
        left = d_ref[pl.ds(first, 8), :width]
        right = d_ref[pl.ds(first, 8), width:]
        turned = pltpu.roll(left, lax.rem(width - first, width), 1)
        columns = [jnp.broadcast_to(turned[:, j : j + 1], (8, width)) for j in range(8)]
        for j in range(8):
            scale = lax.rsqrt(columns[j][j : j + 1, :])
            factor = columns[j] * scale
            for m in range(j + 1, 8):
                columns[m] = columns[m] - factor * factor[m : m + 1, :]
            row_left, row_right = left[j : j + 1, :] * scale, right[j : j + 1, :] * scale
            below, here = strip > j, strip == j
            left = jnp.where(here, row_left, jnp.where(below, left - factor * row_left, left))
            right = jnp.where(here, row_right, jnp.where(below, right - factor * row_right, right))
        later = jnp.where(lane >= first + 8, left, 0.0)
        both = jnp.concatenate([left, right], axis=1)
        d_ref[pl.ds(first, 8), :] = both
        d_ref[...] = d_ref[...] - short_dot(later, both)
        return 0

    for k in range(size // width):
        top, end = k * width, (k + 1) * width
        d_ref[:, :width] = a_ref[top:end, top:end]
        d_ref[:, width:] = small_eye
        lax.fori_loop(0, width // 8, group, 0)
        corner = d_ref[:, width:]
        done = jnp.dot(corner, x_ref[top:end, :end], precision=HIGHEST)
        x_ref[top:end, :end] = done
        if end < size:
            panel = jnp.dot(corner, a_ref[top:end, end:], precision=HIGHEST)
            a_ref[end:, end:] = a_ref[end:, end:] - dot_first(panel, panel)
            x_ref[end:, :end] = x_ref[end:, :end] - dot_first(panel, done)


def lower_inverse(gram_total):
    size = gram_total.shape[0]
    width = 128
    return pl.pallas_call(
        functools.partial(inverse_kernel, size, width),
        out_shape=jax.ShapeDtypeStruct((size, size), jnp.float32),
        in_specs=[pl.BlockSpec(memory_space=pltpu.VMEM)],
        out_specs=pl.BlockSpec(memory_space=pltpu.VMEM),
        scratch_shapes=[
            pltpu.VMEM((size, size), jnp.float32),
            pltpu.VMEM((width, 2 * width), jnp.float32),
        ],
        compiler_params=pltpu.CompilerParams(vmem_limit_bytes=24 * 2**20),
        name="lower_inverse",
    )(gram_total)


def per_device(sizes, momentum, grad, q_basis):
    own_rows = momentum.shape[0]
    basis_rows, rank = q_basis.shape
    devices = math.prod(sizes)
    features = basis_rows * devices
    blended = momentum + grad.astype(jnp.float32)
    blended_low = blended.astype(jnp.bfloat16)
    basis = gather(q_basis.astype(jnp.bfloat16), sizes, 0)
    projected = jnp.dot(blended_low, basis, preferred_element_type=jnp.float32)
    local_gram = jnp.dot(projected.T, projected, precision=HIGHEST)
    gram_total = gather(reduce_scatter(local_gram, sizes, 1), sizes, 2)
    inverse = lower_inverse(gram_total)
    orthonormal = jnp.dot(projected, inverse.T, precision=HIGHEST)
    ortho_low = orthonormal.astype(jnp.bfloat16)
    terms = jnp.dot(blended_low.T, ortho_low, preferred_element_type=jnp.float32)
    summed = reduce_scatter(terms.astype(jnp.bfloat16), sizes, 3)
    summed_low = gather(summed.astype(jnp.bfloat16), sizes, 4)
    wide = summed_low.astype(jnp.float32)
    column_rms = jnp.sqrt(jnp.mean(wide * wide, axis=0) + epsilon)
    q_next = summed / column_rms
    stacked = jnp.concatenate(
        [ortho_low, (orthonormal / column_rms).astype(jnp.bfloat16)], axis=0
    )
    result = jnp.dot(stacked, summed_low.T, preferred_element_type=jnp.float32)
    total_rows = own_rows * devices
    momentum_next = blended - (1.0 - damping) * result[:own_rows]
    update = (math.sqrt(total_rows * features / rank) * result[own_rows:]).astype(jnp.bfloat16)
    return (momentum_next, update, q_next)


def solution(mesh):
    spec = P(("mat", "fsdp"), None)
    return jax.shard_map(
        functools.partial(per_device, grid_of(mesh)),
        mesh=mesh,
        in_specs=(spec, spec, spec),
        out_specs=(spec, spec, spec),
        check_vma=False,
    )
```

profile of v0, /device:TPU:0, one launch (start us, length us, event | category | flops | bytes accessed | tf_op | source)
XLA Modules:
  0.0 220.7 jit_solution(11925746592079891714)
XLA Ops:
  0.6 0.0 copy-start
  0.6 1.2 convert_element_type.30.x_ref
  1.9 51.4 %gather_0.1 = bf16[4,2,2,256,512]{4,3,2,1,0:T(8,128)(2,1)S(1)} custom-call(bf16[256,512]{1,0:T(8,128)(2,1)S(1)} %convert_element_type.30.x_ref), custom_call_target="tpu_custom_call" | custom-call | tf_op jit(solution)/shard_map/gather_0/pallas_call | solution.py:143
  53.2 0.0 copy-done
  53.2 2.8 %fusion.9 = f32[256,512]{1,0:T(8,128)S(1)} fusion(bf16[4096,512]{1,0:T(8,128)(2,1)S(1)} %bitcast.14, f32[256,4096]{1,0:T(8,128)S(1)} %copy-done, bf16[256,4096]{1,0:T(8,128)(2,1)} %param.4), kind=kOutput, calls=%fused_computation.16 | convolution fusion | flops 1076887552 | bytes 11010048 | tf_op jit(solution)/shard_map/dot_general | solution.py:375
  56.1 0.0 copy-start.1
  56.1 1.0 fusion.12
  57.1 20.3 %reduce_1.1.x_ref = f32[32,512]{1,0:T(8,128)S(1)} custom-call(f32[4,2,2,32,512]{4,3,2,1,0:T(8,128)S(1)} %bitcast.16), custom_call_target="tpu_custom_call" | custom-call | tf_op jit(solution)/shard_map/reduce_1/pallas_call | solution.py:262
  77.4 18.8 %gather_2.1 = f32[4,2,2,32,512]{4,3,2,1,0:T(8,128)S(1)} custom-call(f32[32,512]{1,0:T(8,128)S(1)} %reduce_1.1.x_ref), custom_call_target="tpu_custom_call" | custom-call | tf_op jit(solution)/shard_map/gather_2/pallas_call | solution.py:143
  96.2 30.7 %lower_inverse.1 = f32[512,512]{1,0:T(8,128)S(1)} custom-call(f32[512,512]{1,0:T(8,128)S(1)} %bitcast.15), custom_call_target="tpu_custom_call" | custom-call | tf_op jit(solution)/shard_map/lower_inverse/pallas_call | solution.py:353
  126.9 1.1 fusion.11
  128.0 0.0 copy-done.1
  128.0 1.3 convolution_convert_fusion
  129.3 46.7 %reduce_3.1 = f32[256,512]{1,0:T(8,128)S(1)} custom-call(bf16[4,2,2,256,512]{4,3,2,1,0:T(8,128)(2,1)S(1)} %bitcast.13), custom_call_target="tpu_custom_call" | custom-call | tf_op jit(solution)/shard_map/reduce_3/pallas_call | solution.py:262
  176.0 34.6 %gather_4.1 = bf16[4,2,2,256,512]{4,3,2,1,0:T(8,128)(2,1)S(1)} custom-call(bf16[256,512]{1,0:T(8,128)(2,1)S(1)} %convert_element_type.33.x_ref), custom_call_target="tpu_custom_call" | custom-call | tf_op jit(solution)/shard_map/gather_4/pallas_call | solution.py:143
  210.6 1.0 multiply_reduce_fusion
  211.6 0.9 broadcast_divide_fusion
  212.5 2.4 %fusion.3 = f32[512,4096]{1,0:T(8,128)S(1)} fusion(bf16[4096,512]{1,0:T(8,128)(2,1)S(1)} %bitcast.12, bf16[256,512]{1,0:T(8,128)(2,1)S(1)} %get-tuple-element.6, bf16[256,512]{1,0:T(8,128)(2,1)S(1)} %get-tuple-element.7), kind=kOutput, calls=%fused_computation.8 | convolution fusion | flops 2148532224 | bytes 13107200 | tf_op jit(solution)/shard_map/dot_general | solution.py:390
  214.9 5.8 %fusion = (bf16[256,4096]{1,0:T(8,128)(2,1)}, f32[256,4096]{1,0:T(8,128)}) fusion(f32[512,4096]{1,0:T(8,128)S(1)} %fusion.3, f32[256,4096]{1,0:T(8,128)S(1)} %copy-done, bf16[256,4096]{1,0:T(8,128)(2,1)} %param.4), kind=kLoop, calls=%fused_computation.3 | loop fusion | flops 6291456 | bytes 20971520 | tf_op jit(solution)/shard_map/convert_element_type | solution.py:393
  (2 shorter events, 0.0 us)
Async XLA Ops:
  0.6 52.6 %copy-start = (f32[256,4096]{1,0:T(8,128)S(1)}, f32[256,4096]{1,0:T(8,128)}, u32[]{:S(2)}) copy-start(f32[256,4096]{1,0:T(8,128)} %param.3) | copy-start | bytes 12582916
  56.1 71.9 %copy-start.1 = (bf16[256,4096]{1,0:T(8,128)(2,1)S(1)}, bf16[256,4096]{1,0:T(8,128)(2,1)}, u32[]{:S(2)}) copy-start(bf16[256,4096]{1,0:T(8,128)(2,1)} %param.4) | copy-start | bytes 6291460
where the time goes:
time: 224 us; the launch traced here: 221 us
  Pallas kernels  202 us (90%)
  other arithmetic  8.96 us (4%)
  matrix products  8.6 us (4%)
    pallas_call x3, Pallas kernels, gather(): pl.pallas_call(functools.partial(gather_kernel, sizes, pieces), out_shape...  105 us
    pallas_call x2, Pallas kernels, reduce_scatter(): pl.pallas_call(functools.partial(reduce_kernel, sizes, pieces), out_shape...  67 us
    pallas_call x1, Pallas kernels, lower_inverse(): pl.pallas_call(functools.partial(inverse_kernel, size, width), out_shape=...  30.7 us
    convert_element_type x1, other arithmetic, per_device(): (math.sqrt(total_rows * features / rank) * result[own_rows:]).astype(jnp....  5.83 us

commit v1 on v0

--- a/solution.py
+++ b/solution.py
@@ -295,17 +295,17 @@
     )
 
 
-def inverse_kernel(size, width, g_ref, x_ref, a_ref, d_ref):
-    eye = lax.broadcasted_iota(jnp.int32, (size, size), 0) == lax.broadcasted_iota(
-        jnp.int32, (size, size), 1
-    )
-    gram = g_ref[...]
-    trace = jnp.sum(jnp.where(eye, gram, 0.0), keepdims=True)
-    a_ref[...] = gram + jnp.where(eye, 0.0001 * trace / size, 0.0)
-    x_ref[...] = jnp.where(eye, 1.0, 0.0)
+def nt_dot(left, right, precision=None):
+    return lax.dot_general(
+        left, right, (((1,), (1,)), ((), ())), precision=precision, preferred_element_type=jnp.float32
+    )
+
+
+def factor_block(width, d_ref, block):
     strip = lax.broadcasted_iota(jnp.int32, (8, width), 0)
     lane = lax.broadcasted_iota(jnp.int32, (8, width), 1)
-    small_eye = jnp.where(
+    d_ref[:, :width] = block
+    d_ref[:, width:] = jnp.where(
         lax.broadcasted_iota(jnp.int32, (width, width), 0)
         == lax.broadcasted_iota(jnp.int32, (width, width), 1),
         1.0,
@@ -333,6 +333,363 @@
         d_ref[...] = d_ref[...] - short_dot(later, both)
         return 0
 
+    lax.fori_loop(0, width // 8, group, 0)
+    return d_ref[:, width:]
+
+
+def block_pieces(rank, width, sizes):
+    long_axis = max(range(3), key=lambda d: sizes[d])
+    first, second = [d for d in range(3) if d != long_axis]
+    pieces = []
+    for k in range(rank // width):
+        half = width // 2
+        pieces.append((k * width, half, (long_axis, first, second), k))
+        pieces.append((k * width + half, half, (long_axis, second, first), k))
+    return pieces
+
+
+def factor_kernel(sizes, pieces, width, g_ref, p_ref, b_ref, o_ref, t_ref, q_ref, *scratch):
+    mine = position(sizes)
+    count = len(pieces)
+    landing = scratch[: 3 * count]
+    sums = scratch[3 * count : 5 * count]
+    a_ref, x_ref, d_ref, terms, ot_ref, own_ref, rs_send, rs_recv, ag_send, ag_recv = scratch[5 * count :]
+    size = g_ref.shape[0]
+    blocks = size // width
+    devices = math.prod(sizes)
+    features = b_ref.shape[1] // devices
+    rows = b_ref.shape[0]
+    greet(mine, sizes)
+    sent = []
+
+    def push(source, target, sems, p, phase, d, off):
+        copy = pltpu.make_async_remote_copy(
+            src_ref=source,
+            dst_ref=target,
+            send_sem=sems[0].at[p, phase, off],
+            recv_sem=sems[1].at[p, phase, off],
+            device_id=device_at(mine, sizes, d, shifted(mine, sizes, d, off)),
+            device_id_type=MESH,
+        )
+        copy.start()
+        sent.append(copy)
+
+    def send(p, phase, d, off, source):
+        push(source, landing[3 * p + phase].at[off - 1], (rs_send, rs_recv), p, phase, d, off)
+
+    def arrive(p, phase, d):
+        for off in range(1, sizes[d]):
+            here = landing[3 * p + phase].at[off - 1]
+            pltpu.make_async_copy(here, here, rs_recv.at[p, phase, off]).wait()
+
+    def begin(p, start, part, order):
+        d = order[2]
+        for off in range(1, sizes[d]):
+            index = [slice(None)] * 3
+            index[d] = shifted(mine, sizes, d, off)
+            send(p, 0, d, off, terms.at[index[0], index[1], index[2], pl.ds(start, part)])
+
+    def first_sums(p, start, part, order):
+        a, b, c = order
+        arrive(p, 0, c)
+        low, high = min(a, b), max(a, b)
+        for off in list(range(1, sizes[b])) + [0]:
+            at_b = shifted(mine, sizes, b, off)
+
+            def one(at_a, _, off=off, at_b=at_b):
+                index = [None] * 3
+                index[a], index[b], index[c] = at_a, at_b, mine[c]
+                total = terms[index[0], index[1], index[2], pl.ds(start, part)].astype(jnp.float32)
+                for k in range(sizes[c] - 1):
+                    total += landing[3 * p][k, index[low], index[high]].astype(jnp.float32)
+                if off:
+                    sums[2 * p][off - 1, at_a] = total.astype(terms.dtype)
+                else:
+                    sums[2 * p + 1][at_a] = total
+                return 0
+
+            lax.fori_loop(0, sizes[a], one, 0)
+        for off in range(1, sizes[b]):
+            send(p, 1, b, off, sums[2 * p].at[off - 1])
+
+    def second_sums(p, start, part, order):
+        a, b, c = order
+        arrive(p, 1, b)
+        for off in list(range(1, sizes[a])) + [0]:
+            at_a = shifted(mine, sizes, a, off)
+            total = sums[2 * p + 1][at_a]
+            for k in range(sizes[b] - 1):
+                total += landing[3 * p + 1][k, at_a].astype(jnp.float32)
+            if off:
+                landing[3 * p + 2][sizes[a] - 1 + off - 1] = total.astype(terms.dtype)
+            else:
+                sums[2 * p + 1][at_a] = total
+        for off in range(1, sizes[a]):
+            send(p, 2, a, off, landing[3 * p + 2].at[sizes[a] - 1 + off - 1])
+
+    def block(p, phase, coordinate):
+        start, part, order, _ = pieces[p]
+        index = list(mine)
+        index[order[phase]] = coordinate
+        for d in order[:phase]:
+            index[d] = slice(None)
+        return o_ref.at[index[0], index[1], index[2], pl.ds(start, part)]
+
+    def spread(p, phase):
+        d = pieces[p][2][phase]
+        here = block(p, phase, mine[d])
+        for off in range(1, sizes[d]):
+            push(here, here, (ag_send, ag_recv), p, phase, d, off)
+
+    def gathered(p, phase):
+        d = pieces[p][2][phase]
+        for off in range(1, sizes[d]):
+            landed = block(p, phase, shifted(mine, sizes, d, sizes[d] - off))
+            pltpu.make_async_copy(landed, landed, ag_recv.at[p, phase, off]).wait()
+
+    def last_sums(p, start, part, order):
+        a = order[0]
+        arrive(p, 2, a)
+        total = sums[2 * p + 1][mine[a]]
+        for k in range(sizes[a] - 1):
+            total += landing[3 * p + 2][k].astype(jnp.float32)
+        own_ref[pl.ds(start, part), :] = total
+        o_ref[mine[0], mine[1], mine[2], pl.ds(start, part)] = total.astype(o_ref.dtype)
+        spread(p, 0)
+
+    def pass_on(phase):
+        def stage(p, start, part, order):
+            gathered(p, phase - 1)
+            spread(p, phase)
+
+        return stage
+
+    def finish(p, start, part, order):
+        gathered(p, 2)
+
+    stages = (begin, first_sums, second_sums, last_sums, pass_on(1), pass_on(2), finish)
+
+    def serve(k, stage):
+        for p, piece in enumerate(pieces):
+            if piece[3] == k:
+                stages[stage](p, *piece[:3])
+        if stage == len(stages) - 1:
+            scale_block(k)
+
+    def scale_block(k):
+        top, end = k * width, (k + 1) * width
+
+        def squares(i, total):
+            at = (lax.div(i, sizes[1] * sizes[2]), lax.rem(lax.div(i, sizes[2]), sizes[1]), lax.rem(i, sizes[2]))
+            wide = o_ref[at[0], at[1], at[2], top:end].astype(jnp.float32)
+            return total + wide * wide
+
+        total = lax.fori_loop(0, devices, squares, jnp.zeros((width, features), jnp.float32))
+        mean = jnp.sum(total, axis=1, keepdims=True) / (devices * features)
+        column_rms = jnp.sqrt(mean + epsilon)
+        q_ref[top:end, :] = own_ref[top:end, :] / column_rms
+        t_ref[rows:, top:end] = (ot_ref[top:end, :] / column_rms).T.astype(t_ref.dtype)
+
+    def factor(k):
+        top, end = k * width, (k + 1) * width
+        corner = factor_block(width, d_ref, a_ref[top:end, top:end])
+        done = jnp.dot(corner, x_ref[top:end, :end], precision=HIGHEST)
+        x_ref[top:end, :end] = done
+        ortho = nt_dot(done, p_ref[:, :end], HIGHEST)
+        ot_ref[top:end, :] = ortho
+        t_ref[:rows, top:end] = ortho.T.astype(t_ref.dtype)
+        low = ortho.astype(jnp.bfloat16)
+
+        def one(i, _):
+            at = (lax.div(i, sizes[1] * sizes[2]), lax.rem(lax.div(i, sizes[2]), sizes[1]), lax.rem(i, sizes[2]))
+            lanes = pl.ds(pl.multiple_of(i * features, features), features)
+            term = jnp.dot(low, b_ref[:, lanes], preferred_element_type=jnp.float32)
+            terms[at[0], at[1], at[2], top:end] = term.astype(terms.dtype)
+            return 0
+
+        lax.fori_loop(0, devices, one, 0)
+        serve(k, 0)
+        if end < size:
+            panel = jnp.dot(corner, a_ref[top:end, end:], precision=HIGHEST)
+            a_ref[end:, end:] = a_ref[end:, end:] - dot_first(panel, panel)
+            x_ref[end:, :end] = x_ref[end:, :end] - dot_first(panel, done)
+
+    eye = lax.broadcasted_iota(jnp.int32, (size, size), 0) == lax.broadcasted_iota(
+        jnp.int32, (size, size), 1
+    )
+    gram = g_ref[...]
+    trace = jnp.sum(jnp.where(eye, gram, 0.0), keepdims=True)
+    a_ref[...] = gram + jnp.where(eye, 0.0001 * trace / size, 0.0)
+    x_ref[...] = jnp.where(eye, 1.0, 0.0)
+    for slot in range(blocks + len(stages) - 1):
+        if slot < blocks:
+            factor(slot)
+        for k in range(min(slot, blocks)):
+            if 0 < slot - k < len(stages):
+                serve(k, slot - k)
+    for copy in sent:
+        copy.wait_send()
+
+
+def right_factor(gram_total, projected, blended_low, sizes, number):
+    size = gram_total.shape[0]
+    rows, columns = blended_low.shape
+    width = 128
+    devices = math.prod(sizes)
+    features = columns // devices
+    pieces = block_pieces(size, width, sizes)
+    low_type = jnp.bfloat16
+    landing, sums = [], []
+    many = lambda k: max(k, 1)
+    for _, part, (a, b, c), _ in pieces:
+        low, high = min(a, b), max(a, b)
+        landing += [
+            pltpu.VMEM((many(sizes[c] - 1), sizes[low], sizes[high], part, features), low_type),
+            pltpu.VMEM((many(sizes[b] - 1), sizes[a], part, features), low_type),
+            pltpu.VMEM((many(2 * (sizes[a] - 1)), part, features), low_type),
+        ]
+        sums += [
+            pltpu.VMEM((many(sizes[b] - 1), sizes[a], part, features), low_type),
+            pltpu.VMEM((sizes[a], part, features), jnp.float32),
+        ]
+    sems = pltpu.SemaphoreType.DMA((len(pieces), 3, max(sizes)))
+    vmem = pl.BlockSpec(memory_space=pltpu.VMEM)
+    return pl.pallas_call(
+        functools.partial(factor_kernel, sizes, pieces, width),
+        out_shape=(
+            jax.ShapeDtypeStruct(sizes + (size, features), low_type),
+            jax.ShapeDtypeStruct((2 * rows, size), low_type),
+            jax.ShapeDtypeStruct((size, features), jnp.float32),
+        ),
+        in_specs=[vmem, vmem, vmem],
+        out_specs=(vmem, vmem, vmem),
+        scratch_shapes=landing
+        + sums
+        + [
+            pltpu.VMEM((size, size), jnp.float32),
+            pltpu.VMEM((size, size), jnp.float32),
+            pltpu.VMEM((width, 2 * width), jnp.float32),
+            pltpu.VMEM(sizes + (size, features), low_type),
+            pltpu.VMEM((size, rows), jnp.float32),
+            pltpu.VMEM((size, features), jnp.float32),
+            sems,
+            sems,
+            sems,
+            sems,
+        ],
+        compiler_params=pltpu.CompilerParams(
+            collective_id=number, has_side_effects=True, vmem_limit_bytes=40 * 2**20
+        ),
+        name=f"factor_{number}",
+    )(gram_total, projected, blended_low)
+
+
+def finish_kernel(step, factor, s_ref, t_ref, q_ref, m_ref, g_ref, mo_ref, uo_ref, qo_ref, m_buf, u_buf, q_buf, m_sem, u_sem, q_sem):
+    rows = m_ref.shape[0]
+    blocks, rank, features = s_ref.shape
+    q_buf[...] = q_ref[...].T
+    q_copy = pltpu.make_async_copy(q_buf, qo_ref, q_sem)
+    q_copy.start()
+
+    def copies(slot, i):
+        lanes = pl.ds(pl.multiple_of(i * features, features), features)
+        return (
+            pltpu.make_async_copy(m_buf.at[slot], mo_ref.at[:, lanes], m_sem.at[slot]),
+            pltpu.make_async_copy(u_buf.at[slot], uo_ref.at[:, lanes], u_sem.at[slot]),
+        )
+
+    slots = m_buf.shape[0]
+
+    def one(i, _):
+        slot = lax.rem(i, slots)
+
+        @pl.when(i >= slots)
+        def _():
+            for copy in copies(slot, i - slots):
+                copy.wait()
+
+        lanes = pl.ds(pl.multiple_of(i * features, features), features)
+        result = jnp.dot(t_ref[...], s_ref[i], preferred_element_type=jnp.float32)
+        blended = m_ref[:, lanes] + g_ref[:, lanes].astype(jnp.float32)
+        m_buf[slot] = blended - step * result[:rows]
+        u_buf[slot] = (factor * result[rows:]).astype(u_buf.dtype)
+        for copy in copies(slot, i):
+            copy.start()
+        return 0
+
+    lax.fori_loop(0, blocks, one, 0)
+    for i in range(max(blocks - slots, 0), blocks):
+        for copy in copies(i % slots, i):
+            copy.wait()
+    q_copy.wait()
+
+
+def finish(spread, stacked, turned, momentum, grad, factor):
+    rows, columns = momentum.shape
+    blocks, rank, features = spread.shape
+    vmem = pl.BlockSpec(memory_space=pltpu.VMEM)
+    anywhere = pl.BlockSpec(memory_space=pl.ANY)
+    slots = 4
+    return pl.pallas_call(
+        functools.partial(finish_kernel, 1.0 - damping, factor),
+        out_shape=(
+            jax.ShapeDtypeStruct((rows, columns), jnp.float32),
+            jax.ShapeDtypeStruct((rows, columns), jnp.bfloat16),
+            jax.ShapeDtypeStruct((features, rank), jnp.float32),
+        ),
+        in_specs=[vmem] * 5,
+        out_specs=(anywhere,) * 3,
+        scratch_shapes=[
+            pltpu.VMEM((slots, rows, features), jnp.float32),
+            pltpu.VMEM((slots, rows, features), jnp.bfloat16),
+            pltpu.VMEM((features, rank), jnp.float32),
+            pltpu.SemaphoreType.DMA((slots,)),
+            pltpu.SemaphoreType.DMA((slots,)),
+            pltpu.SemaphoreType.DMA,
+        ],
+        compiler_params=pltpu.CompilerParams(vmem_limit_bytes=16 * 2**20),
+        name="finish",
+    )(spread, stacked, turned, momentum, grad)
+
+
+def inverse_kernel(size, width, g_ref, x_ref, a_ref, d_ref):
+    eye = lax.broadcasted_iota(jnp.int32, (size, size), 0) == lax.broadcasted_iota(
+        jnp.int32, (size, size), 1
+    )
+    gram = g_ref[...]
+    trace = jnp.sum(jnp.where(eye, gram, 0.0), keepdims=True)
+    a_ref[...] = gram + jnp.where(eye, 0.0001 * trace / size, 0.0)
+    x_ref[...] = jnp.where(eye, 1.0, 0.0)
+    strip = lax.broadcasted_iota(jnp.int32, (8, width), 0)
+    lane = lax.broadcasted_iota(jnp.int32, (8, width), 1)
+    small_eye = jnp.where(
+        lax.broadcasted_iota(jnp.int32, (width, width), 0)
+        == lax.broadcasted_iota(jnp.int32, (width, width), 1),
+        1.0,
+        0.0,
+    )
+
+    def group(g, _):
+        first = pl.multiple_of(g * 8, 8)
+        left = d_ref[pl.ds(first, 8), :width]
+        right = d_ref[pl.ds(first, 8), width:]
+        turned = pltpu.roll(left, lax.rem(width - first, width), 1)
+        columns = [jnp.broadcast_to(turned[:, j : j + 1], (8, width)) for j in range(8)]
+        for j in range(8):
+            scale = lax.rsqrt(columns[j][j : j + 1, :])
+            factor = columns[j] * scale
+            for m in range(j + 1, 8):
+                columns[m] = columns[m] - factor * factor[m : m + 1, :]
+            row_left, row_right = left[j : j + 1, :] * scale, right[j : j + 1, :] * scale
+            below, here = strip > j, strip == j
+            left = jnp.where(here, row_left, jnp.where(below, left - factor * row_left, left))
+            right = jnp.where(here, row_right, jnp.where(below, right - factor * row_right, right))
+        later = jnp.where(lane >= first + 8, left, 0.0)
+        both = jnp.concatenate([left, right], axis=1)
+        d_ref[pl.ds(first, 8), :] = both
+        d_ref[...] = d_ref[...] - short_dot(later, both)
+        return 0
+
     for k in range(size // width):
         top, end = k * width, (k + 1) * width
         d_ref[:, :width] = a_ref[top:end, top:end]
@@ -364,7 +721,7 @@
     )(gram_total)
 
 
-def per_device(sizes, momentum, grad, q_basis):
+def narrow_device(sizes, momentum, grad, q_basis):
     own_rows = momentum.shape[0]
     basis_rows, rank = q_basis.shape
     devices = math.prod(sizes)
@@ -394,6 +751,26 @@
     return (momentum_next, update, q_next)
 
 
+def per_device(sizes, momentum, grad, q_basis):
+    own_rows = momentum.shape[0]
+    basis_rows, rank = q_basis.shape
+    if basis_rows % 128 or rank % 128:
+        return narrow_device(sizes, momentum, grad, q_basis)
+    devices = math.prod(sizes)
+    features = basis_rows * devices
+    blended = momentum + grad.astype(jnp.float32)
+    blended_low = blended.astype(jnp.bfloat16)
+    basis = gather(q_basis.astype(jnp.bfloat16), sizes, 0)
+    projected = jnp.dot(blended_low, basis, preferred_element_type=jnp.float32)
+    local_gram = jnp.dot(projected.T, projected, precision=HIGHEST)
+    gram_total = gather(reduce_scatter(local_gram, sizes, 1), sizes, 2)
+    spread, stacked, turned = right_factor(gram_total, projected, blended_low, sizes, 3)
+    total_rows = own_rows * devices
+    factor = math.sqrt(total_rows * features / rank)
+    spread = spread.reshape(devices, rank, basis_rows)
+    return finish(spread, stacked, turned, momentum, grad, factor)
+
+
 def solution(mesh):
     spec = P(("mat", "fsdp"), None)
     return jax.shard_map(

time: 224 us -> 205 us (0.915); the launches traced: 221 us -> 204 us
  matrix products: 8.6 us -> 2.28 us
  Pallas kernels: 202 us -> 197 us
  other arithmetic: 8.96 us -> 4.49 us
    pallas_call x1 -> x2, Pallas kernels: 30.7 us -> 107 us  [the longest x1 101 us: right_factor(): pl.pallas_call(functools.partial(factor_kernel, sizes, pieces, width), ou...]
    pallas_call x2 -> x1, Pallas kernels: 67 us -> 20.3 us  [reduce_scatter(): pl.pallas_call(functools.partial(reduce_kernel, sizes, pieces), out_shape...]
    pallas_call x3 -> x2, Pallas kernels: 105 us -> 70.1 us  [gather(): pl.pallas_call(functools.partial(gather_kernel, sizes, pieces), out_shape...]
    dot_general x3 -> x0, matrix products: 4.73 us -> none  [the longest x1 2.37 us: per_device(): result = jnp.dot(stacked, summed_low.T, preferred_element_type=jnp.float32)]
    convert_element_type x2 -> x1, other arithmetic: 5.86 us -> 3.42 us  [per_device(): blended_low = blended.astype(jnp.bfloat16)]
where the time goes in v1:
time: 205 us; the launch traced here: 204 us
  Pallas kernels  197 us (96%)
  other arithmetic  4.49 us (2%)
  matrix products  2.28 us (1%)
    pallas_call x1, Pallas kernels, right_factor(): pl.pallas_call(functools.partial(factor_kernel, sizes, pieces, width), ou...  101 us
    pallas_call x2, Pallas kernels, gather(): pl.pallas_call(functools.partial(gather_kernel, sizes, pieces), out_shape...  70.1 us
    pallas_call x1, Pallas kernels, reduce_scatter(): pl.pallas_call(functools.partial(reduce_kernel, sizes, pieces), out_shape...  20.3 us
    pallas_call x1, Pallas kernels, finish(): pl.pallas_call(functools.partial(finish_kernel, 1.0 - damping, factor), o...  5.8 us

profile of v1, /device:TPU:0, one launch (start us, length us, event | category | flops | bytes accessed | tf_op | source)
XLA Modules:
  0.0 204.5 jit_solution(17550330648217449881)
XLA Ops:
  0.6 1.1 convert_element_type.11.x_ref
  1.7 3.4 %add_convert_fusion.b_ref = bf16[256,4096]{1,0:T(8,128)(2,1)S(1)} fusion(f32[256,4096]{1,0:T(8,128)} %m_ref.1, bf16[256,4096]{1,0:T(8,128)(2,1)} %g_ref.1), kind=kLoop, calls=%fused_computation | loop fusion | flops 3145728 | bytes 8388608 | tf_op jit(solution)/shard_map/convert_element_type | solution.py:762
  5.1 51.4 %gather_0.1 = bf16[4,2,2,256,512]{4,3,2,1,0:T(8,128)(2,1)S(1)} custom-call(bf16[256,512]{1,0:T(8,128)(2,1)S(1)} %convert_element_type.11.x_ref), custom_call_target="tpu_custom_call" | custom-call | tf_op jit(solution)/shard_map/gather_0/pallas_call | solution.py:143
  56.5 1.2 fusion.p_ref
  57.7 0.0 copy-start
  57.8 0.0 copy-start.1
  57.8 1.0 fusion.1
  58.8 20.3 %reduce_1.1.x_ref = f32[32,512]{1,0:T(8,128)S(1)} custom-call(f32[4,2,2,32,512]{4,3,2,1,0:T(8,128)S(1)} %bitcast.10), custom_call_target="tpu_custom_call" | custom-call | tf_op jit(solution)/shard_map/reduce_1/pallas_call | solution.py:262
  79.1 18.8 %gather_2.1 = f32[4,2,2,32,512]{4,3,2,1,0:T(8,128)S(1)} custom-call(f32[32,512]{1,0:T(8,128)S(1)} %reduce_1.1.x_ref), custom_call_target="tpu_custom_call" | custom-call | tf_op jit(solution)/shard_map/gather_2/pallas_call | solution.py:143
  97.9 100.8 %factor_3.1 = (bf16[4,2,2,512,256]{4,3,2,1,0:T(8,128)(2,1)S(1)}, bf16[512,512]{1,0:T(8,128)(2,1)S(1)}, f32[512,256]{1,0:T(8,128)S(1)}) custom-call(f32[512,512]{1,0:T(8,128)S(1)} %bitcast.8, f32[256,512]{1,0:T(8,128)S(1)} %fusion.p_ref, bf16[256,4096]{1,0:T(8,128)(2,1)S(1)} %add_convert_fusion.b_ref), custom_call_target="tpu_custom_call" | custom-call | tf_op jit(solution)/shard_map/factor_3/pallas_call | solution.py:557
  198.7 0.0 copy-done
  198.7 0.0 copy-done.1
  198.7 5.8 %finish.1 = (f32[256,4096]{1,0:T(8,128)}, bf16[256,4096]{1,0:T(8,128)(2,1)}, f32[256,512]{1,0:T(8,128)}) custom-call(bf16[16,512,256]{2,1,0:T(8,128)(2,1)S(1)} %bitcast.11, bf16[512,512]{1,0:T(8,128)(2,1)S(1)} %get-tuple-element.7.t_ref, f32[512,256]{1,0:T(8,128)S(1)} %get-tuple-element.8.q_ref, f32[256,4096]{1,0:T(8,128)S(1)} %copy-done, ...), custom_call_target="tpu_custom_call" | custom-call | tf_op jit(solution)/shard_map/finish/pallas_call | solution.py:633
Async XLA Ops:
  57.7 140.9 %copy-start = (f32[256,4096]{1,0:T(8,128)S(1)}, f32[256,4096]{1,0:T(8,128)}, u32[]{:S(2)}) copy-start(f32[256,4096]{1,0:T(8,128)} %m_ref.1) | copy-start | bytes 12582916
  57.8 140.9 %copy-start.1 = (bf16[256,4096]{1,0:T(8,128)(2,1)S(1)}, bf16[256,4096]{1,0:T(8,128)(2,1)}, u32[]{:S(2)}) copy-start(bf16[256,4096]{1,0:T(8,128)(2,1)} %g_ref.1) | copy-start | bytes 6291460

commit v2 on v1

--- a/solution.py
+++ b/solution.py
@@ -337,61 +337,160 @@
     return d_ref[:, width:]
 
 
-def block_pieces(rank, width, sizes):
+def split(rows, unit, sizes, k):
+    units = rows // unit
     long_axis = max(range(3), key=lambda d: sizes[d])
-    first, second = [d for d in range(3) if d != long_axis]
-    pieces = []
-    for k in range(rank // width):
-        half = width // 2
-        pieces.append((k * width, half, (long_axis, first, second), k))
-        pieces.append((k * width + half, half, (long_axis, second, first), k))
+    one, two = [d for d in range(3) if d != long_axis]
+    if k % 2:
+        one, two = two, one
+    tail = units // 8
+    share, extra = divmod(units - tail, 2)
+    plan = ((tail, (one, two, long_axis)), (share + extra, (long_axis, one, two)), (share, (long_axis, two, one)))
+    pieces, start = [], 0
+    for count, order in plan:
+        if count:
+            pieces.append((start, count * unit, order))
+        start += count * unit
     return pieces
 
 
-def factor_kernel(sizes, pieces, width, g_ref, p_ref, b_ref, o_ref, t_ref, q_ref, *scratch):
+def flows_of(blocks, width, basis_rows, sizes):
+    long_axis = max(range(3), key=lambda d: sizes[d])
+    one, two = [d for d in range(3) if d != long_axis]
+    devices = math.prod(sizes)
+    flows = []
+    for k in range(blocks):
+        flows += [("q", k) + piece for piece in split(basis_rows, 16, sizes, k)]
+    for k in range(blocks):
+        order = (long_axis, one, two) if k % 2 else (long_axis, two, one)
+        flows.append(("g", k, 0, (k + 1) * width // devices, order))
+    for k in range(blocks):
+        flows += [("s", k, k * width + start, rows, order) for start, rows, order in split(width, 16, sizes, k)]
+    return flows
+
+
+def agenda(blocks):
+    steps = []
+    for k in range(blocks):
+        for stage in range(4):
+            steps.append((9.0 * k + (0, 6, 10, 16)[stage], 0, "q", k, stage))
+        if k < blocks - 1:
+            for stage in range(7):
+                steps.append((9.0 * k + 17 + 3.0 * stage, 1, "g", k, stage))
+    begun = 9.0 * (blocks - 1) + 17
+    steps.append((begun + 0.1, 2, "trace", 0, 0))
+    for k in range(blocks):
+        start = begun + 4 + 8.5 * k
+        steps.append((start, 3, "factor", k, 0))
+        for stage in range(7):
+            steps.append((start + 8.5 * stage + 0.1, 4, "s", k, stage))
+    last = (0, 3, 12.4, 12.45, 20.9, 20.95, 29.4)
+    for stage in range(7):
+        steps.append((begun + last[stage], 1, "g", blocks - 1, stage))
+    order = [step[2:] for step in sorted(steps)]
+    for k in range(blocks):
+        at = order.index(("factor", k, 0))
+        late = [step for step in order[at:] if step[:2] == ("g", k)]
+        order = [step for step in order if step not in late]
+        at = order.index(("factor", k, 0))
+        order[at:at] = late
+    return order
+
+
+def main_kernel(sizes, flows, width, m_ref, g_ref, q_ref, o_ref, t_ref, qn_ref, *scratch):
     mine = position(sizes)
-    count = len(pieces)
-    landing = scratch[: 3 * count]
-    sums = scratch[3 * count : 5 * count]
-    a_ref, x_ref, d_ref, terms, ot_ref, own_ref, rs_send, rs_recv, ag_send, ag_recv = scratch[5 * count :]
-    size = g_ref.shape[0]
+    me = lax.axis_index("fsdp")
+    devices = math.prod(sizes)
+    rows, columns = m_ref.shape
+    features, size = q_ref.shape
     blocks = size // width
-    devices = math.prod(sizes)
-    features = b_ref.shape[1] // devices
-    rows = b_ref.shape[0]
-    greet(mine, sizes)
+    refs = list(scratch)
+    take = lambda n: [refs.pop(0) for _ in range(n)]
+    landing, sums = {}, {}
+    for f, flow in enumerate(flows):
+        if flow[0] != "q":
+            landing[f] = take(3)
+            sums[f] = take(2)
+    grams = take(blocks)
+    spreads = take(blocks)
+    (m_buf, g_buf, q_buf, b_ref, basis, p_ref, trace_own, trace_all, u_ref, x_ref, d_ref) = take(11)
+    (terms, ot_ref, own_ref, gram_ref) = take(4)
+    (in_sem, trace_send, trace_recv, rs_send, rs_recv, ag_send, ag_recv) = take(7)
+    base = [0, sizes[0] - 1, sizes[0] + sizes[1] - 2]
+    each = sum(sizes) - 3
+
+    loads = [
+        pltpu.make_async_copy(q_ref, q_buf, in_sem.at[0]),
+        pltpu.make_async_copy(m_ref, m_buf, in_sem.at[1]),
+        pltpu.make_async_copy(g_ref, g_buf, in_sem.at[2]),
+    ]
+    for load in loads:
+        load.start()
+    barrier = pltpu.get_barrier_semaphore()
+    for off in range(1, devices):
+        other = {"fsdp": lax.rem(me + off, devices)}
+        pl.semaphore_signal(barrier, inc=1, device_id=other, device_id_type=MESH)
+    loads[0].wait()
+    for k in range(blocks):
+        basis[k, mine[0], mine[1], mine[2]] = q_buf[:, k * width : (k + 1) * width].astype(basis.dtype)
+    pl.semaphore_wait(barrier, devices - 1)
     sent = []
 
-    def push(source, target, sems, p, phase, d, off):
+    def push(source, target, sems, f, d, off):
+        at = each * f + base[d] + off - 1
         copy = pltpu.make_async_remote_copy(
             src_ref=source,
             dst_ref=target,
-            send_sem=sems[0].at[p, phase, off],
-            recv_sem=sems[1].at[p, phase, off],
+            send_sem=sems[0].at[at],
+            recv_sem=sems[1].at[at],
             device_id=device_at(mine, sizes, d, shifted(mine, sizes, d, off)),
             device_id_type=MESH,
         )
         copy.start()
         sent.append(copy)
 
-    def send(p, phase, d, off, source):
-        push(source, landing[3 * p + phase].at[off - 1], (rs_send, rs_recv), p, phase, d, off)
-
-    def arrive(p, phase, d):
+    def landed(ref, sem, f, d, off):
+        pltpu.make_async_copy(ref, ref, sem.at[each * f + base[d] + off - 1]).wait()
+
+    def block(f, phase, coordinate):
+        kind, k, start, part, order = flows[f]
+        index = list(mine)
+        index[order[phase]] = coordinate
+        for d in order[:phase]:
+            index[d] = slice(None)
+        if kind == "q":
+            return basis.at[k, index[0], index[1], index[2], pl.ds(start, part)]
+        target = spreads[k] if kind == "g" else o_ref
+        return target.at[index[0], index[1], index[2], pl.ds(start, part)]
+
+    def spread(f, phase):
+        d = flows[f][4][phase]
+        here = block(f, phase, mine[d])
         for off in range(1, sizes[d]):
-            here = landing[3 * p + phase].at[off - 1]
-            pltpu.make_async_copy(here, here, rs_recv.at[p, phase, off]).wait()
-
-    def begin(p, start, part, order):
+            push(here, here, (ag_send, ag_recv), f, d, off)
+
+    def gathered(f, phase):
+        d = flows[f][4][phase]
+        for off in range(1, sizes[d]):
+            landed(block(f, phase, shifted(mine, sizes, d, sizes[d] - off)), ag_recv, f, d, off)
+
+    def source(f):
+        return grams[flows[f][1]] if flows[f][0] == "g" else terms
+
+    def begin(f):
+        _, _, start, part, order = flows[f]
         d = order[2]
         for off in range(1, sizes[d]):
             index = [slice(None)] * 3
             index[d] = shifted(mine, sizes, d, off)
-            send(p, 0, d, off, terms.at[index[0], index[1], index[2], pl.ds(start, part)])
-
-    def first_sums(p, start, part, order):
-        a, b, c = order
-        arrive(p, 0, c)
+            piece = source(f).at[index[0], index[1], index[2], pl.ds(start, part)]
+            push(piece, landing[f][0].at[off - 1], (rs_send, rs_recv), f, d, off)
+
+    def first_sums(f):
+        _, _, start, part, (a, b, c) = flows[f]
+        from_ref = source(f)
+        for off in range(1, sizes[c]):
+            landed(landing[f][0].at[off - 1], rs_recv, f, c, off)
         low, high = min(a, b), max(a, b)
         for off in list(range(1, sizes[b])) + [0]:
             at_b = shifted(mine, sizes, b, off)
@@ -399,189 +498,273 @@
             def one(at_a, _, off=off, at_b=at_b):
                 index = [None] * 3
                 index[a], index[b], index[c] = at_a, at_b, mine[c]
-                total = terms[index[0], index[1], index[2], pl.ds(start, part)].astype(jnp.float32)
+                total = from_ref[index[0], index[1], index[2], pl.ds(start, part)].astype(jnp.float32)
                 for k in range(sizes[c] - 1):
-                    total += landing[3 * p][k, index[low], index[high]].astype(jnp.float32)
+                    total += landing[f][0][k, index[low], index[high]].astype(jnp.float32)
                 if off:
-                    sums[2 * p][off - 1, at_a] = total.astype(terms.dtype)
+                    sums[f][0][off - 1, at_a] = total.astype(from_ref.dtype)
                 else:
-                    sums[2 * p + 1][at_a] = total
+                    sums[f][1][at_a] = total
                 return 0
 
             lax.fori_loop(0, sizes[a], one, 0)
         for off in range(1, sizes[b]):
-            send(p, 1, b, off, sums[2 * p].at[off - 1])
-
-    def second_sums(p, start, part, order):
-        a, b, c = order
-        arrive(p, 1, b)
+            push(sums[f][0].at[off - 1], landing[f][1].at[off - 1], (rs_send, rs_recv), f, b, off)
+
+    def second_sums(f):
+        _, _, start, part, (a, b, c) = flows[f]
+        for off in range(1, sizes[b]):
+            landed(landing[f][1].at[off - 1], rs_recv, f, b, off)
+        last = landing[f][2]
         for off in list(range(1, sizes[a])) + [0]:
             at_a = shifted(mine, sizes, a, off)
-            total = sums[2 * p + 1][at_a]
+            total = sums[f][1][at_a]
             for k in range(sizes[b] - 1):
-                total += landing[3 * p + 1][k, at_a].astype(jnp.float32)
+                total += landing[f][1][k, at_a].astype(jnp.float32)
             if off:
-                landing[3 * p + 2][sizes[a] - 1 + off - 1] = total.astype(terms.dtype)
+                last[sizes[a] - 1 + off - 1] = total.astype(last.dtype)
             else:
-                sums[2 * p + 1][at_a] = total
+                sums[f][1][at_a] = total
         for off in range(1, sizes[a]):
-            send(p, 2, a, off, landing[3 * p + 2].at[sizes[a] - 1 + off - 1])
-
-    def block(p, phase, coordinate):
-        start, part, order, _ = pieces[p]
-        index = list(mine)
-        index[order[phase]] = coordinate
-        for d in order[:phase]:
-            index[d] = slice(None)
-        return o_ref.at[index[0], index[1], index[2], pl.ds(start, part)]
-
-    def spread(p, phase):
-        d = pieces[p][2][phase]
-        here = block(p, phase, mine[d])
-        for off in range(1, sizes[d]):
-            push(here, here, (ag_send, ag_recv), p, phase, d, off)
-
-    def gathered(p, phase):
-        d = pieces[p][2][phase]
-        for off in range(1, sizes[d]):
-            landed = block(p, phase, shifted(mine, sizes, d, sizes[d] - off))
-            pltpu.make_async_copy(landed, landed, ag_recv.at[p, phase, off]).wait()
-
-    def last_sums(p, start, part, order):
-        a = order[0]
-        arrive(p, 2, a)
-        total = sums[2 * p + 1][mine[a]]
-        for k in range(sizes[a] - 1):
-            total += landing[3 * p + 2][k].astype(jnp.float32)
-        own_ref[pl.ds(start, part), :] = total
-        o_ref[mine[0], mine[1], mine[2], pl.ds(start, part)] = total.astype(o_ref.dtype)
-        spread(p, 0)
-
-    def pass_on(phase):
-        def stage(p, start, part, order):
-            gathered(p, phase - 1)
-            spread(p, phase)
-
-        return stage
-
-    def finish(p, start, part, order):
-        gathered(p, 2)
-
-    stages = (begin, first_sums, second_sums, last_sums, pass_on(1), pass_on(2), finish)
-
-    def serve(k, stage):
-        for p, piece in enumerate(pieces):
-            if piece[3] == k:
-                stages[stage](p, *piece[:3])
-        if stage == len(stages) - 1:
-            scale_block(k)
+            push(last.at[sizes[a] - 1 + off - 1], last.at[off - 1], (rs_send, rs_recv), f, a, off)
+
+    def last_sums(f):
+        kind, k, start, part, (a, b, c) = flows[f]
+        for off in range(1, sizes[a]):
+            landed(landing[f][2].at[off - 1], rs_recv, f, a, off)
+        total = sums[f][1][mine[a]]
+        for n in range(sizes[a] - 1):
+            total += landing[f][2][n].astype(jnp.float32)
+        if kind == "s":
+            own_ref[pl.ds(start, part), :] = total
+            o_ref[mine[0], mine[1], mine[2], pl.ds(start, part)] = total.astype(o_ref.dtype)
+        else:
+            spreads[k][mine[0], mine[1], mine[2]] = total
+
+    def spot(i):
+        return (
+            lax.div(i, sizes[1] * sizes[2]),
+            lax.rem(lax.div(i, sizes[2]), sizes[1]),
+            lax.rem(i, sizes[2]),
+        )
+
+    def lanes_of(i):
+        return pl.ds(pl.multiple_of(i * features, features), features)
+
+    def blend():
+        loads[1].wait()
+        loads[2].wait()
+
+        def one(i, _):
+            lanes = lanes_of(i)
+            b_ref[:, lanes] = (m_buf[:, lanes] + g_buf[:, lanes].astype(jnp.float32)).astype(b_ref.dtype)
+            return 0
+
+        lax.fori_loop(0, devices, one, 0)
+
+    def project(k):
+        top, end = k * width, (k + 1) * width
+
+        def one(i, total):
+            at = spot(i)
+            return total + jnp.dot(
+                b_ref[:, lanes_of(i)], basis[k, at[0], at[1], at[2]], preferred_element_type=jnp.float32
+            )
+
+        p_ref[:, top:end] = lax.fori_loop(0, devices, one, jnp.zeros((rows, width), jnp.float32))
+        column = dot_first(p_ref[:, :end], p_ref[:, top:end])
+        part = end // devices
+        for i in range(devices):
+            at = (i // (sizes[1] * sizes[2]), i // sizes[2] % sizes[1], i % sizes[2])
+            grams[k][at[0], at[1], at[2]] = column[i * part : (i + 1) * part]
+
+    def send_trace():
+        square = p_ref[...] * p_ref[...]
+        folded = square[:, :128]
+        for i in range(1, size // 128):
+            folded = folded + square[:, i * 128 : (i + 1) * 128]
+        tile = folded[:8]
+        for i in range(1, rows // 8):
+            tile = tile + folded[i * 8 : (i + 1) * 8]
+        trace_own[...] = tile
+        trace_all[me] = tile
+        for off in range(1, devices):
+            copy = pltpu.make_async_remote_copy(
+                src_ref=trace_own,
+                dst_ref=trace_all.at[me],
+                send_sem=trace_send.at[off],
+                recv_sem=trace_recv.at[off],
+                device_id={"fsdp": lax.rem(me + off, devices)},
+                device_id_type=MESH,
+            )
+            copy.start()
+            sent.append(copy)
+
+    def ridge():
+        for off in range(1, devices):
+            here = trace_all.at[lax.rem(me + devices - off, devices)]
+            pltpu.make_async_copy(here, here, trace_recv.at[off]).wait()
+        return jnp.sum(jnp.sum(trace_all[...], axis=0), keepdims=True) * (0.0001 / size)
+
+    small_eye = lax.broadcasted_iota(jnp.int32, (width, width), 0) == lax.broadcasted_iota(
+        jnp.int32, (width, width), 1
+    )
+    shared = {}
+
+    def factor(k):
+        top, end = k * width, (k + 1) * width
+        if k == 0:
+            shared["ridge"] = ridge()
+        gram_ref[:end, :] = spreads[k][...].reshape(end, width)
+        for j in range(k):
+            near, far = j * width, (j + 1) * width
+            upper = gram_ref[near:far, :]
+            if j:
+                upper = upper - dot_first(u_ref[:near, near:far], u_ref[:near, top:end])
+            u_ref[near:far, top:end] = jnp.dot(x_ref[near:far, near:far], upper, precision=HIGHEST)
+        corner = gram_ref[top:end, :] + jnp.where(small_eye, shared["ridge"], 0.0)
+        if k:
+            panel = u_ref[:top, top:end]
+            corner = corner - dot_first(panel, panel)
+        inverse = factor_block(width, d_ref, corner)
+        x_ref[top:end, top:end] = inverse
+        if k:
+            rest = dot_first(u_ref[:top, top:end], x_ref[:top, :top])
+            x_ref[top:end, :top] = -jnp.dot(inverse, rest, precision=HIGHEST)
+        if end < size:
+            x_ref[top:end, end:] = jnp.zeros((width, size - end), jnp.float32)
+        ortho = nt_dot(x_ref[top:end, :end], p_ref[:, :end], HIGHEST)
+        ot_ref[top:end, :] = ortho
+        t_ref[:rows, top:end] = ortho.T.astype(t_ref.dtype)
+        low = ortho.astype(jnp.bfloat16)
+
+        def one(i, _):
+            at = spot(i)
+            term = jnp.dot(low, b_ref[:, lanes_of(i)], preferred_element_type=jnp.float32)
+            terms[at[0], at[1], at[2], top:end] = term.astype(terms.dtype)
+            return 0
+
+        lax.fori_loop(0, devices, one, 0)
 
     def scale_block(k):
         top, end = k * width, (k + 1) * width
 
         def squares(i, total):
-            at = (lax.div(i, sizes[1] * sizes[2]), lax.rem(lax.div(i, sizes[2]), sizes[1]), lax.rem(i, sizes[2]))
+            at = spot(i)
             wide = o_ref[at[0], at[1], at[2], top:end].astype(jnp.float32)
             return total + wide * wide
 
         total = lax.fori_loop(0, devices, squares, jnp.zeros((width, features), jnp.float32))
         mean = jnp.sum(total, axis=1, keepdims=True) / (devices * features)
         column_rms = jnp.sqrt(mean + epsilon)
-        q_ref[top:end, :] = own_ref[top:end, :] / column_rms
+        qn_ref[top:end, :] = own_ref[top:end, :] / column_rms
         t_ref[rows:, top:end] = (ot_ref[top:end, :] / column_rms).T.astype(t_ref.dtype)
 
-    def factor(k):
-        top, end = k * width, (k + 1) * width
-        corner = factor_block(width, d_ref, a_ref[top:end, top:end])
-        done = jnp.dot(corner, x_ref[top:end, :end], precision=HIGHEST)
-        x_ref[top:end, :end] = done
-        ortho = nt_dot(done, p_ref[:, :end], HIGHEST)
-        ot_ref[top:end, :] = ortho
-        t_ref[:rows, top:end] = ortho.T.astype(t_ref.dtype)
-        low = ortho.astype(jnp.bfloat16)
-
-        def one(i, _):
-            at = (lax.div(i, sizes[1] * sizes[2]), lax.rem(lax.div(i, sizes[2]), sizes[1]), lax.rem(i, sizes[2]))
-            lanes = pl.ds(pl.multiple_of(i * features, features), features)
-            term = jnp.dot(low, b_ref[:, lanes], preferred_element_type=jnp.float32)
-            terms[at[0], at[1], at[2], top:end] = term.astype(terms.dtype)
-            return 0
-
-        lax.fori_loop(0, devices, one, 0)
-        serve(k, 0)
-        if end < size:
-            panel = jnp.dot(corner, a_ref[top:end, end:], precision=HIGHEST)
-            a_ref[end:, end:] = a_ref[end:, end:] - dot_first(panel, panel)
-            x_ref[end:, :end] = x_ref[end:, :end] - dot_first(panel, done)
-
-    eye = lax.broadcasted_iota(jnp.int32, (size, size), 0) == lax.broadcasted_iota(
-        jnp.int32, (size, size), 1
-    )
-    gram = g_ref[...]
-    trace = jnp.sum(jnp.where(eye, gram, 0.0), keepdims=True)
-    a_ref[...] = gram + jnp.where(eye, 0.0001 * trace / size, 0.0)
-    x_ref[...] = jnp.where(eye, 1.0, 0.0)
-    for slot in range(blocks + len(stages) - 1):
-        if slot < blocks:
-            factor(slot)
-        for k in range(min(slot, blocks)):
-            if 0 < slot - k < len(stages):
-                serve(k, slot - k)
+    def serve(kind, k, stage):
+        mine_flows = [f for f, flow in enumerate(flows) if flow[:2] == (kind, k)]
+        if kind != "q":
+            for f in mine_flows:
+                if stage < 4:
+                    (begin, first_sums, second_sums, last_sums)[stage](f)
+            stage = stage - 4
+            if stage < -1:
+                return
+            if stage == -1:
+                for f in mine_flows:
+                    spread(f, 0)
+                return
+            stage = stage + 1
+        for f in mine_flows:
+            if stage:
+                gathered(f, stage - 1)
+            if stage < 3:
+                spread(f, stage)
+        if stage == 3 and kind == "q":
+            project(k)
+        if stage == 3 and kind == "s":
+            scale_block(k)
+
+    blended = False
+    for kind, k, stage in agenda(blocks):
+        if kind == "trace":
+            send_trace()
+        elif kind == "factor":
+            factor(k)
+        else:
+            serve(kind, k, stage)
+        if not blended and kind == "q" and stage == 0:
+            blend()
+            blended = True
     for copy in sent:
         copy.wait_send()
 
 
-def right_factor(gram_total, projected, blended_low, sizes, number):
-    size = gram_total.shape[0]
-    rows, columns = blended_low.shape
+def right_factor(momentum, grad, q_basis, sizes, number):
+    rows, columns = momentum.shape
+    features, size = q_basis.shape
     width = 128
+    blocks = size // width
     devices = math.prod(sizes)
-    features = columns // devices
-    pieces = block_pieces(size, width, sizes)
+    flows = flows_of(blocks, width, features, sizes)
     low_type = jnp.bfloat16
-    landing, sums = [], []
     many = lambda k: max(k, 1)
-    for _, part, (a, b, c), _ in pieces:
+    scratch = []
+    for kind, _, _, part, (a, b, c) in flows:
+        if kind == "q":
+            continue
         low, high = min(a, b), max(a, b)
-        landing += [
-            pltpu.VMEM((many(sizes[c] - 1), sizes[low], sizes[high], part, features), low_type),
-            pltpu.VMEM((many(sizes[b] - 1), sizes[a], part, features), low_type),
-            pltpu.VMEM((many(2 * (sizes[a] - 1)), part, features), low_type),
+        lanes, kept = (width, jnp.float32) if kind == "g" else (features, low_type)
+        scratch += [
+            pltpu.VMEM((many(sizes[c] - 1), sizes[low], sizes[high], part, lanes), kept),
+            pltpu.VMEM((many(sizes[b] - 1), sizes[a], part, lanes), kept),
+            pltpu.VMEM((many(2 * (sizes[a] - 1)), part, lanes), kept),
+            pltpu.VMEM((many(sizes[b] - 1), sizes[a], part, lanes), kept),
+            pltpu.VMEM((sizes[a], part, lanes), jnp.float32),
         ]
-        sums += [
-            pltpu.VMEM((many(sizes[b] - 1), sizes[a], part, features), low_type),
-            pltpu.VMEM((sizes[a], part, features), jnp.float32),
-        ]
-    sems = pltpu.SemaphoreType.DMA((len(pieces), 3, max(sizes)))
+    parts = [pltpu.VMEM(sizes + ((k + 1) * width // devices, width), jnp.float32) for k in range(blocks)]
+    sems = pltpu.SemaphoreType.DMA((len(flows) * (sum(sizes) - 3),))
+    scratch += parts + parts
+    scratch += [
+        pltpu.VMEM((rows, columns), jnp.float32),
+        pltpu.VMEM((rows, columns), low_type),
+        pltpu.VMEM((features, size), jnp.float32),
+        pltpu.VMEM((rows, columns), low_type),
+        pltpu.VMEM((blocks,) + sizes + (features, width), low_type),
+        pltpu.VMEM((rows, size), jnp.float32),
+        pltpu.VMEM((8, 128), jnp.float32),
+        pltpu.VMEM((devices, 8, 128), jnp.float32),
+        pltpu.VMEM((size, size), jnp.float32),
+        pltpu.VMEM((size, size), jnp.float32),
+        pltpu.VMEM((width, 2 * width), jnp.float32),
+        pltpu.VMEM(sizes + (size, features), low_type),
+        pltpu.VMEM((size, rows), jnp.float32),
+        pltpu.VMEM((size, features), jnp.float32),
+        pltpu.VMEM((size, width), jnp.float32),
+        pltpu.SemaphoreType.DMA((3,)),
+        pltpu.SemaphoreType.DMA((devices,)),
+        pltpu.SemaphoreType.DMA((devices,)),
+        sems,
+        sems,
+        sems,
+        sems,
+    ]
     vmem = pl.BlockSpec(memory_space=pltpu.VMEM)
+    anywhere = pl.BlockSpec(memory_space=pl.ANY)
     return pl.pallas_call(
-        functools.partial(factor_kernel, sizes, pieces, width),
+        functools.partial(main_kernel, sizes, flows, width),
         out_shape=(
             jax.ShapeDtypeStruct(sizes + (size, features), low_type),
             jax.ShapeDtypeStruct((2 * rows, size), low_type),
             jax.ShapeDtypeStruct((size, features), jnp.float32),
         ),
-        in_specs=[vmem, vmem, vmem],
+        in_specs=[anywhere] * 3,
         out_specs=(vmem, vmem, vmem),
-        scratch_shapes=landing
-        + sums
-        + [
-            pltpu.VMEM((size, size), jnp.float32),
-            pltpu.VMEM((size, size), jnp.float32),
-            pltpu.VMEM((width, 2 * width), jnp.float32),
-            pltpu.VMEM(sizes + (size, features), low_type),
-            pltpu.VMEM((size, rows), jnp.float32),
-            pltpu.VMEM((size, features), jnp.float32),
-            sems,
-            sems,
-            sems,
-            sems,
-        ],
+        scratch_shapes=scratch,
         compiler_params=pltpu.CompilerParams(
-            collective_id=number, has_side_effects=True, vmem_limit_bytes=40 * 2**20
+            collective_id=number, has_side_effects=True, vmem_limit_bytes=50 * 2**20
         ),
         name=f"factor_{number}",
-    )(gram_total, projected, blended_low)
+    )(momentum, grad, q_basis)
 
 
 def finish_kernel(step, factor, s_ref, t_ref, q_ref, m_ref, g_ref, mo_ref, uo_ref, qo_ref, m_buf, u_buf, q_buf, m_sem, u_sem, q_sem):
@@ -754,17 +937,11 @@
 def per_device(sizes, momentum, grad, q_basis):
     own_rows = momentum.shape[0]
     basis_rows, rank = q_basis.shape
-    if basis_rows % 128 or rank % 128:
+    if basis_rows % 128 or rank % 128 or own_rows % 128:
         return narrow_device(sizes, momentum, grad, q_basis)
     devices = math.prod(sizes)
     features = basis_rows * devices
-    blended = momentum + grad.astype(jnp.float32)
-    blended_low = blended.astype(jnp.bfloat16)
-    basis = gather(q_basis.astype(jnp.bfloat16), sizes, 0)
-    projected = jnp.dot(blended_low, basis, preferred_element_type=jnp.float32)
-    local_gram = jnp.dot(projected.T, projected, precision=HIGHEST)
-    gram_total = gather(reduce_scatter(local_gram, sizes, 1), sizes, 2)
-    spread, stacked, turned = right_factor(gram_total, projected, blended_low, sizes, 3)
+    spread, stacked, turned = right_factor(momentum, grad, q_basis, sizes, 0)
     total_rows = own_rows * devices
     factor = math.sqrt(total_rows * features / rank)
     spread = spread.reshape(devices, rank, basis_rows)

time: 205 us -> 202 us (0.985)
  local copies, waits for them, and re-layouts: 0.01 us -> 5.1 us
  other arithmetic: 4.49 us -> 0 us
  matrix products: 2.28 us -> 0 us
    unnamed x4 -> x8, local copies, waits for them, and re-layouts: 0.01 us -> 5.1 us
    convert_element_type x2 -> x0, other arithmetic: 4.49 us -> none  [the longest x1 3.42 us: per_device(): blended_low = blended.astype(jnp.bfloat16)]
    dot_general x2 -> x0, matrix products: 2.28 us -> none  [the longest x1 1.24 us: per_device(): projected = jnp.dot(blended_low, basis, preferred_element_type=jnp.float32)]
    pallas_call x4 -> x1, Pallas kernels: 191 us -> 190 us  [right_factor(): pl.pallas_call(functools.partial(main_kernel, sizes, flows, width), out_s...]
where the time goes in v2:
time: 202 us; the launch traced here: 201 us
  Pallas kernels  196 us (97%)
  local copies, waits for them, and re-layouts  5.1 us (3%)
    pallas_call x1, Pallas kernels, right_factor(): pl.pallas_call(functools.partial(main_kernel, sizes, flows, width), out_s...  190 us
    pallas_call x1, Pallas kernels, finish(): pl.pallas_call(functools.partial(finish_kernel, 1.0 - damping, factor), o...  5.8 us
    unnamed x8, local copies, waits for them, and re-layouts  5.1 us

profile of v2, /device:TPU:0, one launch (start us, length us, event | category | flops | bytes accessed | tf_op | source)
XLA Modules:
  0.0 201.4 jit_solution(12421654264106676796)
XLA Ops:
  0.6 0.0 copy-start
  0.6 0.0 copy-start.1
  0.7 1.7 copy-done.1
  2.4 0.0 copy-start.3
  2.4 1.2 copy-done.3
  3.6 189.8 %factor_0.1 = (bf16[4,2,2,512,256]{4,3,2,1,0:T(8,128)(2,1)}, bf16[512,512]{1,0:T(8,128)(2,1)S(1)}, f32[512,256]{1,0:T(8,128)S(1)}) custom-call(f32[256,4096]{1,0:T(8,128)} %m_ref.3, bf16[256,4096]{1,0:T(8,128)(2,1)S(1)} %copy-done.1, f32[256,512]{1,0:T(8,128)S(1)} %copy-done.3), custom_call_target="tpu_custom_call" | custom-call | tf_op jit(solution)/shard_map/factor_0/pallas_call | solution.py:753
  193.4 0.0 copy-done
  193.4 0.0 copy-start.2
  193.4 2.2 %copy-done.2 = bf16[4,2,2,512,256]{4,3,2,1,0:T(8,128)(2,1)S(1)} copy-done((bf16[4,2,2,512,256]{4,3,2,1,0:T(8,128)(2,1)S(1)}, bf16[4,2,2,512,256]{4,3,2,1,0:T(8,128)(2,1)}, u32[]{:S(2)}) %copy-start.2) | copy-done | bytes 4194328
  195.6 5.8 %finish.1 = (f32[256,4096]{1,0:T(8,128)}, bf16[256,4096]{1,0:T(8,128)(2,1)}, f32[256,512]{1,0:T(8,128)}) custom-call(bf16[16,512,256]{2,1,0:T(8,128)(2,1)S(1)} %bitcast.1, bf16[512,512]{1,0:T(8,128)(2,1)S(1)} %get-tuple-element.7.t_ref, f32[512,256]{1,0:T(8,128)S(1)} %get-tuple-element.8.q_ref, f32[256,4096]{1,0:T(8,128)S(1)} %copy-done, ...), custom_call_target="tpu_custom_call" | custom-call | tf_op jit(solution)/shard_map/finish/pallas_call | solution.py:816
Async XLA Ops:
  0.6 192.7 %copy-start = (f32[256,4096]{1,0:T(8,128)S(1)}, f32[256,4096]{1,0:T(8,128)}, u32[]{:S(2)}) copy-start(f32[256,4096]{1,0:T(8,128)} %m_ref.3) | copy-start | bytes 12582916
  0.6 1.7 copy-start.1
  2.4 1.2 copy-start.3
  193.4 2.2 %copy-start.2 = (bf16[4,2,2,512,256]{4,3,2,1,0:T(8,128)(2,1)S(1)}, bf16[4,2,2,512,256]{4,3,2,1,0:T(8,128)(2,1)}, u32[]{:S(2)}) copy-start(bf16[4,2,2,512,256]{4,3,2,1,0:T(8,128)(2,1)} %get-tuple-element.6) | copy-start | bytes 12582916

commit v3 on v2

--- a/solution.py
+++ b/solution.py
@@ -302,8 +302,9 @@
 
 
 def factor_block(width, d_ref, block):
-    strip = lax.broadcasted_iota(jnp.int32, (8, width), 0)
-    lane = lax.broadcasted_iota(jnp.int32, (8, width), 1)
+    group = 32
+    strip = lax.broadcasted_iota(jnp.int32, (group, width), 0)
+    lane = lax.broadcasted_iota(jnp.int32, (group, width), 1)
     d_ref[:, :width] = block
     d_ref[:, width:] = jnp.where(
         lax.broadcasted_iota(jnp.int32, (width, width), 0)
@@ -311,40 +312,36 @@
         1.0,
         0.0,
     )
-
-    def group(g, _):
-        first = pl.multiple_of(g * 8, 8)
-        left = d_ref[pl.ds(first, 8), :width]
-        right = d_ref[pl.ds(first, 8), width:]
-        turned = pltpu.roll(left, lax.rem(width - first, width), 1)
-        columns = [jnp.broadcast_to(turned[:, j : j + 1], (8, width)) for j in range(8)]
-        for j in range(8):
+    for first in range(0, width, group):
+        end = first + group
+        left = d_ref[first:end, :width]
+        right = d_ref[first:end, width:]
+        columns = [
+            jnp.broadcast_to(left[:, first + j : first + j + 1], (group, width)) for j in range(group)
+        ]
+        for j in range(group):
             scale = lax.rsqrt(columns[j][j : j + 1, :])
             factor = columns[j] * scale
-            for m in range(j + 1, 8):
+            for m in range(j + 1, group):
                 columns[m] = columns[m] - factor * factor[m : m + 1, :]
             row_left, row_right = left[j : j + 1, :] * scale, right[j : j + 1, :] * scale
             below, here = strip > j, strip == j
             left = jnp.where(here, row_left, jnp.where(below, left - factor * row_left, left))
             right = jnp.where(here, row_right, jnp.where(below, right - factor * row_right, right))
-        later = jnp.where(lane >= first + 8, left, 0.0)
-        both = jnp.concatenate([left, right], axis=1)
-        d_ref[pl.ds(first, 8), :] = both
-        d_ref[...] = d_ref[...] - short_dot(later, both)
-        return 0
-
-    lax.fori_loop(0, width // 8, group, 0)
+        d_ref[first:end, width:] = right
+        if end < width:
+            later = jnp.where(lane >= end, left, 0.0)
+            both = jnp.concatenate([left, right], axis=1)
+            d_ref[end:, :] = d_ref[end:, :] - short_dot(later, both)[end:]
     return d_ref[:, width:]
 
 
-def split(rows, unit, sizes, k):
-    units = rows // unit
+def split(rows, unit, sizes, k, tail):
     long_axis = max(range(3), key=lambda d: sizes[d])
     one, two = [d for d in range(3) if d != long_axis]
     if k % 2:
         one, two = two, one
-    tail = units // 8
-    share, extra = divmod(units - tail, 2)
+    share, extra = divmod(rows // unit - tail, 2)
     plan = ((tail, (one, two, long_axis)), (share + extra, (long_axis, one, two)), (share, (long_axis, two, one)))
     pieces, start = [], 0
     for count, order in plan:
@@ -360,44 +357,94 @@
     devices = math.prod(sizes)
     flows = []
     for k in range(blocks):
-        flows += [("q", k) + piece for piece in split(basis_rows, 16, sizes, k)]
+        tail = basis_rows // 64 if 0 < k < blocks - 1 else 0
+        flows += [("q", k) + piece for piece in split(basis_rows, 16, sizes, k, tail)]
     for k in range(blocks):
-        order = (long_axis, one, two) if k % 2 else (long_axis, two, one)
+        order = (long_axis, two, one) if k % 2 else (long_axis, one, two)
         flows.append(("g", k, 0, (k + 1) * width // devices, order))
     for k in range(blocks):
-        flows += [("s", k, k * width + start, rows, order) for start, rows, order in split(width, 16, sizes, k)]
+        pieces = split(width, 16, sizes, k, width // 128)
+        flows += [("s", k, k * width + start, rows, order) for start, rows, order in pieces]
     return flows
 
 
-def agenda(blocks):
-    steps = []
+BLEND, PROJECT, TRACE, FACTOR, SCALE = -1, -2, -3, -4, -5
+
+
+TUNED = (
+    0, 20, 21, 10, 50, -10, 1, 60, 11, 70, 51, 2, 61, 30, 40, 80, 12, 31, 22, 41,
+    3, 71, 42, 90, 32, 13, 52, -20, 72, 62, 23, 33, 43, 100, -21, 81, 110, 91, 63, 101,
+    53, 73, 111, -22, 120, 82, 112, 102, 92, 121, 113, 83, 103, 122, 93, -23, 104, 114, -30, 130,
+    123, 105, 124, 131, 115, 106, -40, 116, 125, 160, 140, 150, 132, -41, 141, 180, 126, 133, 170, 161,
+    -42, 151, 134, 162, 142, 190, 181, 200, 135, 171, 152, 191, 220, 136, 163, 210, 143, 153, 182, -43,
+    240, 164, 192, 211, 230, 250, 172, 221, 201, 144, 193, 183, 241, 154, 251, 231, 212, 173, 155, 194,
+    165, 222, 213, 232, 184, 195, 242, 223, 202, 203, 145, 252, 214, 174, 224, 233, 185, 215, 243, 253,
+    234, 156, 166, 225, 244, 204, 254, 235, 175, 245, 226, 146, 186, 255, 196, 205, -50, 236, 176, -51,
+    206, 216, -52, 246, 256, -53,
+)
+
+
+def tuned_agenda(flows, blocks):
+    steps = [divmod(code, 10) if code >= 0 else (-(-code // 10), -code % 10) for code in TUNED]
+    plain = agenda(flows, blocks)
+    return steps if sorted(steps) == sorted(plain) else plain
+
+
+def agenda(flows, blocks):
+    steps = [(0.5, (BLEND, 0))]
+    begun = 9.0 * (blocks - 1) + 17
+    for f, (kind, k, _, _, _) in enumerate(flows):
+        if kind == "q":
+            steps += [(9.0 * k + (0, 6, 10, 16)[stage], (f, stage)) for stage in range(4)]
+        elif kind == "g" and k < blocks - 1:
+            steps += [(9.0 * k + 17.01 + 3.0 * stage, (f, stage)) for stage in range(7)]
+        elif kind == "g":
+            late = (0, 3, 12.9, 13, 21.4, 21.5, 29.9)
+            steps += [(begun + 0.02 + late[stage], (f, stage)) for stage in range(7)]
+        else:
+            steps += [(begun + 4.6 + 8.5 * (k + stage), (f, stage)) for stage in range(7)]
     for k in range(blocks):
-        for stage in range(4):
-            steps.append((9.0 * k + (0, 6, 10, 16)[stage], 0, "q", k, stage))
-        if k < blocks - 1:
-            for stage in range(7):
-                steps.append((9.0 * k + 17 + 3.0 * stage, 1, "g", k, stage))
-    begun = 9.0 * (blocks - 1) + 17
-    steps.append((begun + 0.1, 2, "trace", 0, 0))
+        steps.append((9.0 * k + 16.5, (PROJECT, k)))
+        steps.append((begun + 4 + 8.5 * k, (FACTOR, k)))
+        steps.append((begun + 4.7 + 8.5 * (k + 6), (SCALE, k)))
+    steps.append((begun + 0.1, (TRACE, 0)))
+    steps.sort(key=lambda step: step[0])
+    needs = {}
+    need = lambda step, other: needs.setdefault(step, []).append(other)
+    for f, (kind, k, _, _, _) in enumerate(flows):
+        final = 3 if kind == "q" else 6
+        for stage in range(final):
+            need((f, stage + 1), (f, stage))
+        if kind == "q":
+            need((PROJECT, k), (f, final))
+        elif kind == "g":
+            need((f, 0), (PROJECT, k))
+            need((FACTOR, k), (f, final))
+        else:
+            need((f, 0), (FACTOR, k))
+            need((SCALE, k), (f, final))
     for k in range(blocks):
-        start = begun + 4 + 8.5 * k
-        steps.append((start, 3, "factor", k, 0))
-        for stage in range(7):
-            steps.append((start + 8.5 * stage + 0.1, 4, "s", k, stage))
-    last = (0, 3, 12.4, 12.45, 20.9, 20.95, 29.4)
-    for stage in range(7):
-        steps.append((begun + last[stage], 1, "g", blocks - 1, stage))
-    order = [step[2:] for step in sorted(steps)]
-    for k in range(blocks):
-        at = order.index(("factor", k, 0))
-        late = [step for step in order[at:] if step[:2] == ("g", k)]
-        order = [step for step in order if step not in late]
-        at = order.index(("factor", k, 0))
-        order[at:at] = late
+        need((PROJECT, k), (BLEND, 0))
+        need((TRACE, 0), (PROJECT, k))
+        need((FACTOR, k), (TRACE, 0))
+        if k:
+            need((PROJECT, k), (PROJECT, k - 1))
+            need((FACTOR, k), (FACTOR, k - 1))
+    order, done = [], set()
+
+    def emit(step):
+        if step not in done:
+            for other in needs.get(step, ()):
+                emit(other)
+            done.add(step)
+            order.append(step)
+
+    for _, step in steps:
+        emit(step)
     return order
 
 
-def main_kernel(sizes, flows, width, m_ref, g_ref, q_ref, o_ref, t_ref, qn_ref, *scratch):
+def main_kernel(sizes, flows, width, m_ref, g_ref, q_ref, o_ref, t_ref, qn_ref, m_buf, *scratch):
     mine = position(sizes)
     me = lax.axis_index("fsdp")
     devices = math.prod(sizes)
@@ -413,7 +460,7 @@
             sums[f] = take(2)
     grams = take(blocks)
     spreads = take(blocks)
-    (m_buf, g_buf, q_buf, b_ref, basis, p_ref, trace_own, trace_all, u_ref, x_ref, d_ref) = take(11)
+    (g_buf, q_buf, b_ref, basis, p_ref, trace_own, trace_all, u_ref, x_ref, d_ref) = take(10)
     (terms, ot_ref, own_ref, gram_ref) = take(4)
     (in_sem, trace_send, trace_recv, rs_send, rs_recv, ag_send, ag_recv) = take(7)
     base = [0, sizes[0] - 1, sizes[0] + sizes[1] - 2]
@@ -557,7 +604,9 @@
 
         def one(i, _):
             lanes = lanes_of(i)
-            b_ref[:, lanes] = (m_buf[:, lanes] + g_buf[:, lanes].astype(jnp.float32)).astype(b_ref.dtype)
+            blended = m_buf[:, lanes] + g_buf[:, lanes].astype(jnp.float32)
+            m_buf[:, lanes] = blended
+            b_ref[:, lanes] = blended.astype(b_ref.dtype)
             return 0
 
         lax.fori_loop(0, devices, one, 0)
@@ -660,41 +709,30 @@
         qn_ref[top:end, :] = own_ref[top:end, :] / column_rms
         t_ref[rows:, top:end] = (ot_ref[top:end, :] / column_rms).T.astype(t_ref.dtype)
 
-    def serve(kind, k, stage):
-        mine_flows = [f for f, flow in enumerate(flows) if flow[:2] == (kind, k)]
-        if kind != "q":
-            for f in mine_flows:
-                if stage < 4:
-                    (begin, first_sums, second_sums, last_sums)[stage](f)
-            stage = stage - 4
-            if stage < -1:
+    def serve(f, stage):
+        if flows[f][0] != "q":
+            if stage < 4:
+                (begin, first_sums, second_sums, last_sums)[stage](f)
+            if stage < 3:
                 return
-            if stage == -1:
-                for f in mine_flows:
-                    spread(f, 0)
-                return
-            stage = stage + 1
-        for f in mine_flows:
-            if stage:
-                gathered(f, stage - 1)
-            if stage < 3:
-                spread(f, stage)
-        if stage == 3 and kind == "q":
-            project(k)
-        if stage == 3 and kind == "s":
-            scale_block(k)
-
-    blended = False
-    for kind, k, stage in agenda(blocks):
-        if kind == "trace":
-            send_trace()
-        elif kind == "factor":
-            factor(k)
+            stage = stage - 3
+        if stage:
+            gathered(f, stage - 1)
+        if stage < 3:
+            spread(f, stage)
+
+    special = {
+        BLEND: lambda k: blend(),
+        PROJECT: project,
+        TRACE: lambda k: send_trace(),
+        FACTOR: factor,
+        SCALE: scale_block,
+    }
+    for what, stage in tuned_agenda(flows, blocks):
+        if what < 0:
+            special[what](stage)
         else:
-            serve(kind, k, stage)
-        if not blended and kind == "q" and stage == 0:
-            blend()
-            blended = True
+            serve(what, stage)
     for copy in sent:
         copy.wait_send()
 
@@ -725,7 +763,6 @@
     sems = pltpu.SemaphoreType.DMA((len(flows) * (sum(sizes) - 3),))
     scratch += parts + parts
     scratch += [
-        pltpu.VMEM((rows, columns), jnp.float32),
         pltpu.VMEM((rows, columns), low_type),
         pltpu.VMEM((features, size), jnp.float32),
         pltpu.VMEM((rows, columns), low_type),
@@ -749,25 +786,25 @@
         sems,
     ]
     vmem = pl.BlockSpec(memory_space=pltpu.VMEM)
-    anywhere = pl.BlockSpec(memory_space=pl.ANY)
     return pl.pallas_call(
         functools.partial(main_kernel, sizes, flows, width),
         out_shape=(
             jax.ShapeDtypeStruct(sizes + (size, features), low_type),
             jax.ShapeDtypeStruct((2 * rows, size), low_type),
             jax.ShapeDtypeStruct((size, features), jnp.float32),
+            jax.ShapeDtypeStruct((rows, columns), jnp.float32),
         ),
-        in_specs=[anywhere] * 3,
-        out_specs=(vmem, vmem, vmem),
+        in_specs=[pl.BlockSpec(memory_space=pltpu.HBM)] * 3,
+        out_specs=(vmem, vmem, vmem, vmem),
         scratch_shapes=scratch,
         compiler_params=pltpu.CompilerParams(
-            collective_id=number, has_side_effects=True, vmem_limit_bytes=50 * 2**20
+            collective_id=number, has_side_effects=True, vmem_limit_bytes=40 * 2**20
         ),
         name=f"factor_{number}",
     )(momentum, grad, q_basis)
 
 
-def finish_kernel(step, factor, s_ref, t_ref, q_ref, m_ref, g_ref, mo_ref, uo_ref, qo_ref, m_buf, u_buf, q_buf, m_sem, u_sem, q_sem):
+def finish_kernel(step, factor, s_ref, t_ref, q_ref, m_ref, mo_ref, uo_ref, qo_ref, m_buf, u_buf, q_buf, m_sem, u_sem, q_sem):
     rows = m_ref.shape[0]
     blocks, rank, features = s_ref.shape
     q_buf[...] = q_ref[...].T
@@ -793,8 +830,7 @@
 
         lanes = pl.ds(pl.multiple_of(i * features, features), features)
         result = jnp.dot(t_ref[...], s_ref[i], preferred_element_type=jnp.float32)
-        blended = m_ref[:, lanes] + g_ref[:, lanes].astype(jnp.float32)
-        m_buf[slot] = blended - step * result[:rows]
+        m_buf[slot] = m_ref[:, lanes] - step * result[:rows]
         u_buf[slot] = (factor * result[rows:]).astype(u_buf.dtype)
         for copy in copies(slot, i):
             copy.start()
@@ -807,8 +843,8 @@
     q_copy.wait()
 
 
-def finish(spread, stacked, turned, momentum, grad, factor):
-    rows, columns = momentum.shape
+def finish(spread, stacked, turned, blended, factor):
+    rows, columns = blended.shape
     blocks, rank, features = spread.shape
     vmem = pl.BlockSpec(memory_space=pltpu.VMEM)
     anywhere = pl.BlockSpec(memory_space=pl.ANY)
@@ -820,7 +856,7 @@
             jax.ShapeDtypeStruct((rows, columns), jnp.bfloat16),
             jax.ShapeDtypeStruct((features, rank), jnp.float32),
         ),
-        in_specs=[vmem] * 5,
+        in_specs=[vmem] * 4,
         out_specs=(anywhere,) * 3,
         scratch_shapes=[
             pltpu.VMEM((slots, rows, features), jnp.float32),
@@ -832,7 +868,7 @@
         ],
         compiler_params=pltpu.CompilerParams(vmem_limit_bytes=16 * 2**20),
         name="finish",
-    )(spread, stacked, turned, momentum, grad)
+    )(spread, stacked, turned, blended)
 
 
 def inverse_kernel(size, width, g_ref, x_ref, a_ref, d_ref):
@@ -941,11 +977,11 @@
         return narrow_device(sizes, momentum, grad, q_basis)
     devices = math.prod(sizes)
     features = basis_rows * devices
-    spread, stacked, turned = right_factor(momentum, grad, q_basis, sizes, 0)
+    spread, stacked, turned, blended = right_factor(momentum, grad, q_basis, sizes, 0)
     total_rows = own_rows * devices
     factor = math.sqrt(total_rows * features / rank)
     spread = spread.reshape(devices, rank, basis_rows)
-    return finish(spread, stacked, turned, momentum, grad, factor)
+    return finish(spread, stacked, turned, blended, factor)
 
 
 def solution(mesh):

time: 202 us -> 160 us (0.79)
  Pallas kernels: 196 us -> 157 us
  local copies, waits for them, and re-layouts: 5.1 us -> 2.63 us
    pallas_call x1, Pallas kernels: 190 us -> 151 us  [right_factor(): pl.pallas_call(functools.partial(main_kernel, sizes, flows, width), out_s...]
    unnamed x8 -> x4, local copies, waits for them, and re-layouts: 5.1 us -> 2.63 us
where the time goes in v3:
time: 160 us
  Pallas kernels  157 us (98%)
  local copies, waits for them, and re-layouts  2.63 us (2%)
    pallas_call x1, Pallas kernels, right_factor(): pl.pallas_call(functools.partial(main_kernel, sizes, flows, width), out_s...  151 us
    pallas_call x1, Pallas kernels, finish(): pl.pallas_call(functools.partial(finish_kernel, 1.0 - damping, factor), o...  5.8 us

profile of v3, /device:TPU:0, one launch (start us, length us, event | category | flops | bytes accessed | tf_op | source)
XLA Modules:
  0.0 160.1 jit_solution(151880560849779503)
XLA Ops:
  0.6 0.0 copy-start
  0.6 1.6 copy-done
  2.2 0.0 copy-start.1
  2.2 1.0 copy-done.1
  3.3 150.9 %factor_0.1 = (bf16[4,2,2,512,256]{4,3,2,1,0:T(8,128)(2,1)S(1)}, bf16[512,512]{1,0:T(8,128)(2,1)S(1)}, f32[512,256]{1,0:T(8,128)S(1)}, f32[256,4096]{1,0:T(8,128)S(1)}) custom-call(f32[256,4096]{1,0:T(8,128)} %m_ref.1, bf16[256,4096]{1,0:T(8,128)(2,1)S(1)} %copy-done, f32[256,512]{1,0:T(8,128)S(1)} %copy-done.1), custom_call_target="tpu_custom_call" | custom-call | tf_op jit(solution)/shard_map/factor_0/pallas_call | solution.py:789
  154.1 5.8 %finish.1 = (f32[256,4096]{1,0:T(8,128)}, bf16[256,4096]{1,0:T(8,128)(2,1)}, f32[256,512]{1,0:T(8,128)}) custom-call(bf16[16,512,256]{2,1,0:T(8,128)(2,1)S(1)} %bitcast.1, bf16[512,512]{1,0:T(8,128)(2,1)S(1)} %get-tuple-element.8.t_ref, f32[512,256]{1,0:T(8,128)S(1)} %get-tuple-element.9.q_ref, f32[256,4096]{1,0:T(8,128)S(1)} %get-tuple-element.10.m_ref), custom_call_target="tpu_custom_call" | custom-call | tf_op jit(solution)/shard_map/finish/pallas_call | solution.py:852
Async XLA Ops:
  0.6 1.6 copy-start
  2.2 1.0 copy-start.1

commit v4 on v3

--- a/solution.py
+++ b/solution.py
@@ -368,26 +368,27 @@
     return flows
 
 
-BLEND, PROJECT, TRACE, FACTOR, SCALE = -1, -2, -3, -4, -5
+BLEND, PROJECT, TRACE, FACTOR, SCALE, TELL, HEAR = -1, -2, -3, -4, -5, -6, -7
 
 
 TUNED = (
-    0, 20, 21, 10, 50, -10, 1, 60, 11, 70, 51, 2, 61, 30, 40, 80, 12, 31, 22, 41,
-    3, 71, 42, 90, 32, 13, 52, -20, 72, 62, 23, 33, 43, 100, -21, 81, 110, 91, 63, 101,
-    53, 73, 111, -22, 120, 82, 112, 102, 92, 121, 113, 83, 103, 122, 93, -23, 104, 114, -30, 130,
-    123, 105, 124, 131, 115, 106, -40, 116, 125, 160, 140, 150, 132, -41, 141, 180, 126, 133, 170, 161,
-    -42, 151, 134, 162, 142, 190, 181, 200, 135, 171, 152, 191, 220, 136, 163, 210, 143, 153, 182, -43,
-    240, 164, 192, 211, 230, 250, 172, 221, 201, 144, 193, 183, 241, 154, 251, 231, 212, 173, 155, 194,
-    165, 222, 213, 232, 184, 195, 242, 223, 202, 203, 145, 252, 214, 174, 224, 233, 185, 215, 243, 253,
-    234, 156, 166, 225, 244, 204, 254, 235, 175, 245, 226, 146, 186, 255, 196, 205, -50, 236, 176, -51,
-    206, 216, -52, 246, 256, -53,
+    10, 20, 40, 21, 50, -10, 30, 11, 41, 0, 31, 12, 42, 80, 60, 1, 81, 90, 51, 43,
+    61, 2, 13, 70, 91, 32, 62, 82, 22, 3, 71, 52, -20, 100, 33, 23, -21, 63, 101, 92,
+    72, 110, 83, 102, 73, 53, -22, 93, 103, 120, -23, 130, 111, 121, -30, 112, 104, 122, 131, 105,
+    106, 113, 132, 123, -40, 114, 124, 150, 160, 133, 115, 134, 161, 151, 140, 125, 116, -41, 135, 126,
+    162, 152, 180, 170, 190, -42, 200, 136, 141, 191, 163, 210, 171, 153, 181, -43, 230, 201, 172, 211,
+    250, 182, 240, 220, 142, 192, 164, 154, 212, 241, 251, 202, 183, 242, 173, 155, 231, 143, 184, 213,
+    203, 232, 144, 221, 243, 174, 165, 252, 214, 185, 222, 193, 233, 204, 244, 253, 234, 223, 215, 194,
+    186, 254, 166, 224, 156, 205, 245, 175, 145, 195, 235, 255, 225, 176, 196, -51, 146, 246, 216, -50,
+    256, 236, 206, -53, 226, -52,
 )
 
 
 def tuned_agenda(flows, blocks):
     steps = [divmod(code, 10) if code >= 0 else (-(-code // 10), -code % 10) for code in TUNED]
     plain = agenda(flows, blocks)
-    return steps if sorted(steps) == sorted(plain) else plain
+    known = sorted(step for step in steps if step[0] > TELL)
+    return steps if known == sorted(plain) else plain
 
 
 def agenda(flows, blocks):
@@ -444,7 +445,7 @@
     return order
 
 
-def main_kernel(sizes, flows, width, m_ref, g_ref, q_ref, o_ref, t_ref, qn_ref, m_buf, *scratch):
+def main_kernel(sizes, parts, flows, width, m_ref, g_ref, q_ref, o_ref, t_ref, qn_ref, m_buf, *scratch):
     mine = position(sizes)
     me = lax.axis_index("fsdp")
     devices = math.prod(sizes)
@@ -462,7 +463,7 @@
     spreads = take(blocks)
     (g_buf, q_buf, b_ref, basis, p_ref, trace_own, trace_all, u_ref, x_ref, d_ref) = take(10)
     (terms, ot_ref, own_ref, gram_ref) = take(4)
-    (in_sem, trace_send, trace_recv, rs_send, rs_recv, ag_send, ag_recv) = take(7)
+    (in_sem, trace_send, trace_recv, rs_send, rs_recv, ag_send, ag_recv, pace) = take(8)
     base = [0, sizes[0] - 1, sizes[0] + sizes[1] - 2]
     each = sum(sizes) - 3
 
@@ -477,10 +478,14 @@
     for off in range(1, devices):
         other = {"fsdp": lax.rem(me + off, devices)}
         pl.semaphore_signal(barrier, inc=1, device_id=other, device_id_type=MESH)
+    part = lax.axis_index("mat")
+    paired = parts == 2
+    if paired:
+        pl.semaphore_signal(barrier, inc=1, device_id={"mat": 1 - part}, device_id_type=MESH)
     loads[0].wait()
     for k in range(blocks):
         basis[k, mine[0], mine[1], mine[2]] = q_buf[:, k * width : (k + 1) * width].astype(basis.dtype)
-    pl.semaphore_wait(barrier, devices - 1)
+    pl.semaphore_wait(barrier, devices - 1 + paired)
     sent = []
 
     def push(source, target, sems, f, d, off):
@@ -721,12 +726,28 @@
         if stage < 3:
             spread(f, stage)
 
+    def tell(n):
+        if paired:
+
+            @pl.when(part == n % 2)
+            def _():
+                pl.semaphore_signal(pace.at[n], inc=1, device_id={"mat": 1 - part}, device_id_type=MESH)
+
+    def hear(n):
+        if paired:
+
+            @pl.when(part != n % 2)
+            def _():
+                pl.semaphore_wait(pace.at[n], 1)
+
     special = {
         BLEND: lambda k: blend(),
         PROJECT: project,
         TRACE: lambda k: send_trace(),
         FACTOR: factor,
         SCALE: scale_block,
+        TELL: tell,
+        HEAR: hear,
     }
     for what, stage in tuned_agenda(flows, blocks):
         if what < 0:
@@ -737,7 +758,7 @@
         copy.wait_send()
 
 
-def right_factor(momentum, grad, q_basis, sizes, number):
+def right_factor(momentum, grad, q_basis, sizes, parts, number):
     rows, columns = momentum.shape
     features, size = q_basis.shape
     width = 128
@@ -759,9 +780,9 @@
             pltpu.VMEM((many(sizes[b] - 1), sizes[a], part, lanes), kept),
             pltpu.VMEM((sizes[a], part, lanes), jnp.float32),
         ]
-    parts = [pltpu.VMEM(sizes + ((k + 1) * width // devices, width), jnp.float32) for k in range(blocks)]
+    chunks = [pltpu.VMEM(sizes + ((k + 1) * width // devices, width), jnp.float32) for k in range(blocks)]
     sems = pltpu.SemaphoreType.DMA((len(flows) * (sum(sizes) - 3),))
-    scratch += parts + parts
+    scratch += chunks + chunks
     scratch += [
         pltpu.VMEM((rows, columns), low_type),
         pltpu.VMEM((features, size), jnp.float32),
@@ -784,21 +805,22 @@
         sems,
         sems,
         sems,
+        pltpu.SemaphoreType.REGULAR((4,)),
     ]
     vmem = pl.BlockSpec(memory_space=pltpu.VMEM)
     return pl.pallas_call(
-        functools.partial(main_kernel, sizes, flows, width),
+        functools.partial(main_kernel, sizes, parts, flows, width),
         out_shape=(
-            jax.ShapeDtypeStruct(sizes + (size, features), low_type),
-            jax.ShapeDtypeStruct((2 * rows, size), low_type),
-            jax.ShapeDtypeStruct((size, features), jnp.float32),
-            jax.ShapeDtypeStruct((rows, columns), jnp.float32),
+            pltpu.VMEM(sizes + (size, features), low_type),
+            pltpu.VMEM((2 * rows, size), low_type),
+            pltpu.VMEM((size, features), jnp.float32),
+            pltpu.VMEM((rows, columns), jnp.float32),
         ),
         in_specs=[pl.BlockSpec(memory_space=pltpu.HBM)] * 3,
         out_specs=(vmem, vmem, vmem, vmem),
         scratch_shapes=scratch,
         compiler_params=pltpu.CompilerParams(
-            collective_id=number, has_side_effects=True, vmem_limit_bytes=40 * 2**20
+            collective_id=number, has_side_effects=True, vmem_limit_bytes=48 * 2**20
         ),
         name=f"factor_{number}",
     )(momentum, grad, q_basis)
@@ -819,24 +841,33 @@
         )
 
     slots = m_buf.shape[0]
-
-    def one(i, _):
-        slot = lax.rem(i, slots)
-
-        @pl.when(i >= slots)
-        def _():
-            for copy in copies(slot, i - slots):
-                copy.wait()
-
-        lanes = pl.ds(pl.multiple_of(i * features, features), features)
-        result = jnp.dot(t_ref[...], s_ref[i], preferred_element_type=jnp.float32)
-        m_buf[slot] = m_ref[:, lanes] - step * result[:rows]
-        u_buf[slot] = (factor * result[rows:]).astype(u_buf.dtype)
-        for copy in copies(slot, i):
-            copy.start()
+    wide = math.gcd(blocks, slots // 2)
+
+    def one(step_index, _):
+        for n in range(wide):
+            i = step_index * wide + n
+            slot = lax.rem(i, slots)
+
+            @pl.when(i >= slots)
+            def _(slot=slot, i=i):
+                for copy in copies(slot, i - slots):
+                    copy.wait()
+
+        results = [
+            jnp.dot(t_ref[...], s_ref[step_index * wide + n], preferred_element_type=jnp.float32)
+            for n in range(wide)
+        ]
+        for n in range(wide):
+            i = step_index * wide + n
+            slot = lax.rem(i, slots)
+            lanes = pl.ds(pl.multiple_of(i * features, features), features)
+            m_buf[slot] = m_ref[:, lanes] - step * results[n][:rows]
+            u_buf[slot] = (factor * results[n][rows:]).astype(u_buf.dtype)
+            for copy in copies(slot, i):
+                copy.start()
         return 0
 
-    lax.fori_loop(0, blocks, one, 0)
+    lax.fori_loop(0, blocks // wide, one, 0)
     for i in range(max(blocks - slots, 0), blocks):
         for copy in copies(i % slots, i):
             copy.wait()
@@ -848,7 +879,7 @@
     blocks, rank, features = spread.shape
     vmem = pl.BlockSpec(memory_space=pltpu.VMEM)
     anywhere = pl.BlockSpec(memory_space=pl.ANY)
-    slots = 4
+    slots = 8
     return pl.pallas_call(
         functools.partial(finish_kernel, 1.0 - damping, factor),
         out_shape=(
@@ -970,14 +1001,14 @@
     return (momentum_next, update, q_next)
 
 
-def per_device(sizes, momentum, grad, q_basis):
+def per_device(sizes, parts, momentum, grad, q_basis):
     own_rows = momentum.shape[0]
     basis_rows, rank = q_basis.shape
     if basis_rows % 128 or rank % 128 or own_rows % 128:
         return narrow_device(sizes, momentum, grad, q_basis)
     devices = math.prod(sizes)
     features = basis_rows * devices
-    spread, stacked, turned, blended = right_factor(momentum, grad, q_basis, sizes, 0)
+    spread, stacked, turned, blended = right_factor(momentum, grad, q_basis, sizes, parts, 0)
     total_rows = own_rows * devices
     factor = math.sqrt(total_rows * features / rank)
     spread = spread.reshape(devices, rank, basis_rows)
@@ -987,7 +1018,7 @@
 def solution(mesh):
     spec = P(("mat", "fsdp"), None)
     return jax.shard_map(
-        functools.partial(per_device, grid_of(mesh)),
+        functools.partial(per_device, grid_of(mesh), mesh.shape["mat"]),
         mesh=mesh,
         in_specs=(spec, spec, spec),
         out_specs=(spec, spec, spec),

time: 160 us -> 156 us (0.975)
  local copies, waits for them, and re-layouts: 2.63 us -> 0 us
  Pallas kernels: 157 us -> 155 us
    unnamed x4 -> x0, local copies, waits for them, and re-layouts: 2.63 us -> none
where the time goes in v4:
time: 156 us
  Pallas kernels  155 us (99%)
    pallas_call x1, Pallas kernels, right_factor(): pl.pallas_call(functools.partial(main_kernel, sizes, parts, flows, width)...  151 us
    pallas_call x1, Pallas kernels, finish(): pl.pallas_call(functools.partial(finish_kernel, 1.0 - damping, factor), o...  4.24 us

profile of v4, /device:TPU:0, one launch (start us, length us, event | category | flops | bytes accessed | tf_op | source)
XLA Modules:
  0.0 156.0 jit_solution(9765558963554194308)
XLA Ops:
  0.6 151.0 %factor_0.1 = (bf16[4,2,2,512,256]{4,3,2,1,0:T(8,128)(2,1)S(1)}, bf16[512,512]{1,0:T(8,128)(2,1)S(1)}, f32[512,256]{1,0:T(8,128)S(1)}, f32[256,4096]{1,0:T(8,128)S(1)}) custom-call(f32[256,4096]{1,0:T(8,128)} %m_ref.1, bf16[256,4096]{1,0:T(8,128)(2,1)} %g_ref.1, f32[256,512]{1,0:T(8,128)} %q_ref.1), custom_call_target="tpu_custom_call" | custom-call | tf_op jit(solution)/shard_map/factor_0/pallas_call | solution.py:811
  151.6 4.2 %finish.1 = (f32[256,4096]{1,0:T(8,128)}, bf16[256,4096]{1,0:T(8,128)(2,1)}, f32[256,512]{1,0:T(8,128)}) custom-call(bf16[16,512,256]{2,1,0:T(8,128)(2,1)S(1)} %bitcast.1, bf16[512,512]{1,0:T(8,128)(2,1)S(1)} %get-tuple-element.8.t_ref, f32[512,256]{1,0:T(8,128)S(1)} %get-tuple-element.9.q_ref, f32[256,4096]{1,0:T(8,128)S(1)} %get-tuple-element.10.m_ref), custom_call_target="tpu_custom_call" | custom-call | tf_op jit(solution)/shard_map/finish/pallas_call | solution.py:883

commit v5 on v4

--- a/solution.py
+++ b/solution.py
@@ -466,6 +466,7 @@
     (in_sem, trace_send, trace_recv, rs_send, rs_recv, ag_send, ag_recv, pace) = take(8)
     base = [0, sizes[0] - 1, sizes[0] + sizes[1] - 2]
     each = sum(sizes) - 3
+    basis_flows = sum(flow[0] == "q" for flow in flows)
 
     loads = [
         pltpu.make_async_copy(q_ref, q_buf, in_sem.at[0]),
@@ -488,21 +489,32 @@
     pl.semaphore_wait(barrier, devices - 1 + paired)
     sent = []
 
+    kinds = ("q", "g", "s")
+
     def push(source, target, sems, f, d, off):
-        at = each * f + base[d] + off - 1
+        summing = sems[0] is rs_send
+        at = each * (f - summing * basis_flows) + base[d] + off - 1
+        kind = flows[f][0]
+        if kind == "g":
+            gram_at = each * (2 * (f - basis_flows) + summing) + base[d] + off - 1
+            send_sem = rs_send.at[gram_at]
+        else:
+            send_sem = ag_send.at[kinds.index(kind) + summing]
         copy = pltpu.make_async_remote_copy(
             src_ref=source,
             dst_ref=target,
-            send_sem=sems[0].at[at],
+            send_sem=send_sem,
             recv_sem=sems[1].at[at],
             device_id=device_at(mine, sizes, d, shifted(mine, sizes, d, off)),
             device_id_type=MESH,
         )
         copy.start()
-        sent.append(copy)
+        if kind == "g":
+            sent.append(copy)
 
     def landed(ref, sem, f, d, off):
-        pltpu.make_async_copy(ref, ref, sem.at[each * f + base[d] + off - 1]).wait()
+        at = each * (f - (sem is rs_recv) * basis_flows) + base[d] + off - 1
+        pltpu.make_async_copy(ref, ref, sem.at[at]).wait()
 
     def block(f, phase, coordinate):
         kind, k, start, part, order = flows[f]
@@ -618,14 +630,10 @@
 
     def project(k):
         top, end = k * width, (k + 1) * width
-
-        def one(i, total):
-            at = spot(i)
-            return total + jnp.dot(
-                b_ref[:, lanes_of(i)], basis[k, at[0], at[1], at[2]], preferred_element_type=jnp.float32
-            )
-
-        p_ref[:, top:end] = lax.fori_loop(0, devices, one, jnp.zeros((rows, width), jnp.float32))
+        right = basis[k].reshape(columns, width)
+        p_ref[:, top:end] = jnp.dot(b_ref[...], right, preferred_element_type=jnp.float32)
+        if end == size:
+            send_trace()
         column = dot_first(p_ref[:, :end], p_ref[:, top:end])
         part = end // devices
         for i in range(devices):
@@ -692,13 +700,17 @@
         t_ref[:rows, top:end] = ortho.T.astype(t_ref.dtype)
         low = ortho.astype(jnp.bfloat16)
 
+        each_step = math.gcd(devices, 4)
+
         def one(i, _):
-            at = spot(i)
-            term = jnp.dot(low, b_ref[:, lanes_of(i)], preferred_element_type=jnp.float32)
-            terms[at[0], at[1], at[2], top:end] = term.astype(terms.dtype)
+            for n in range(each_step):
+                at = spot(i * each_step + n)
+                lanes = lanes_of(i * each_step + n)
+                term = jnp.dot(low, b_ref[:, lanes], preferred_element_type=jnp.float32)
+                terms[at[0], at[1], at[2], top:end] = term.astype(terms.dtype)
             return 0
 
-        lax.fori_loop(0, devices, one, 0)
+        lax.fori_loop(0, devices // each_step, one, 0)
 
     def scale_block(k):
         top, end = k * width, (k + 1) * width
@@ -743,7 +755,7 @@
     special = {
         BLEND: lambda k: blend(),
         PROJECT: project,
-        TRACE: lambda k: send_trace(),
+        TRACE: lambda k: None,
         FACTOR: factor,
         SCALE: scale_block,
         TELL: tell,
@@ -754,8 +766,13 @@
             special[what](stage)
         else:
             serve(what, stage)
-    for copy in sent:
-        copy.wait_send()
+        if (what, stage) == (FACTOR, blocks - 1):
+            while sent:
+                sent.pop().wait_send()
+    shares = size // devices * (devices - 1)
+    everything = terms.at[:, :, :, pl.ds(0, shares)]
+    for n in (0, 2, 3):
+        pltpu.make_async_copy(everything, everything, ag_send.at[n]).wait()
 
 
 def right_factor(momentum, grad, q_basis, sizes, parts, number):
@@ -781,7 +798,9 @@
             pltpu.VMEM((sizes[a], part, lanes), jnp.float32),
         ]
     chunks = [pltpu.VMEM(sizes + ((k + 1) * width // devices, width), jnp.float32) for k in range(blocks)]
+    sums_flows = sum(flow[0] != "q" for flow in flows)
     sems = pltpu.SemaphoreType.DMA((len(flows) * (sum(sizes) - 3),))
+    sum_sems = pltpu.SemaphoreType.DMA((sums_flows * (sum(sizes) - 3),))
     scratch += chunks + chunks
     scratch += [
         pltpu.VMEM((rows, columns), low_type),
@@ -801,9 +820,9 @@
         pltpu.SemaphoreType.DMA((3,)),
         pltpu.SemaphoreType.DMA((devices,)),
         pltpu.SemaphoreType.DMA((devices,)),
-        sems,
-        sems,
-        sems,
+        pltpu.SemaphoreType.DMA((2 * blocks * (sum(sizes) - 3),)),
+        sum_sems,
+        pltpu.SemaphoreType.DMA((4,)),
         sems,
         pltpu.SemaphoreType.REGULAR((4,)),
     ]

time: 156 us -> 146 us (0.936)
  Pallas kernels: 155 us -> 145 us
    pallas_call x1, Pallas kernels: 151 us -> 141 us  [right_factor(): pl.pallas_call(functools.partial(main_kernel, sizes, parts, flows, width)...]
where the time goes in v5:
time: 146 us
  Pallas kernels  145 us (99%)
    pallas_call x1, Pallas kernels, right_factor(): pl.pallas_call(functools.partial(main_kernel, sizes, parts, flows, width)...  141 us
    pallas_call x1, Pallas kernels, finish(): pl.pallas_call(functools.partial(finish_kernel, 1.0 - damping, factor), o...  4.24 us

profile of v5, /device:TPU:0, one launch (start us, length us, event | category | flops | bytes accessed | tf_op | source)
XLA Modules:
  0.0 145.7 jit_solution(2261269403471800505)
XLA Ops:
  0.6 140.7 %factor_0.1 = (bf16[4,2,2,512,256]{4,3,2,1,0:T(8,128)(2,1)S(1)}, bf16[512,512]{1,0:T(8,128)(2,1)S(1)}, f32[512,256]{1,0:T(8,128)S(1)}, f32[256,4096]{1,0:T(8,128)S(1)}) custom-call(f32[256,4096]{1,0:T(8,128)} %m_ref.1, bf16[256,4096]{1,0:T(8,128)(2,1)} %g_ref.1, f32[256,512]{1,0:T(8,128)} %q_ref.1), custom_call_target="tpu_custom_call" | custom-call | tf_op jit(solution)/shard_map/factor_0/pallas_call | solution.py:830
  141.3 4.2 %finish.1 = (f32[256,4096]{1,0:T(8,128)}, bf16[256,4096]{1,0:T(8,128)(2,1)}, f32[256,512]{1,0:T(8,128)}) custom-call(bf16[16,512,256]{2,1,0:T(8,128)(2,1)S(1)} %bitcast.1, bf16[512,512]{1,0:T(8,128)(2,1)S(1)} %get-tuple-element.8.t_ref, f32[512,256]{1,0:T(8,128)S(1)} %get-tuple-element.9.q_ref, f32[256,4096]{1,0:T(8,128)S(1)} %get-tuple-element.10.m_ref), custom_call_target="tpu_custom_call" | custom-call | tf_op jit(solution)/shard_map/finish/pallas_call | solution.py:902

commit v6 on v5

--- a/solution.py
+++ b/solution.py
@@ -372,15 +372,15 @@
 
 
 TUNED = (
-    10, 20, 40, 21, 50, -10, 30, 11, 41, 0, 31, 12, 42, 80, 60, 1, 81, 90, 51, 43,
-    61, 2, 13, 70, 91, 32, 62, 82, 22, 3, 71, 52, -20, 100, 33, 23, -21, 63, 101, 92,
-    72, 110, 83, 102, 73, 53, -22, 93, 103, 120, -23, 130, 111, 121, -30, 112, 104, 122, 131, 105,
-    106, 113, 132, 123, -40, 114, 124, 150, 160, 133, 115, 134, 161, 151, 140, 125, 116, -41, 135, 126,
-    162, 152, 180, 170, 190, -42, 200, 136, 141, 191, 163, 210, 171, 153, 181, -43, 230, 201, 172, 211,
-    250, 182, 240, 220, 142, 192, 164, 154, 212, 241, 251, 202, 183, 242, 173, 155, 231, 143, 184, 213,
-    203, 232, 144, 221, 243, 174, 165, 252, 214, 185, 222, 193, 233, 204, 244, 253, 234, 223, 215, 194,
-    186, 254, 166, 224, 156, 205, 245, 175, 145, 195, 235, 255, 225, 176, 196, -51, 146, 246, 216, -50,
-    256, 236, 206, -53, 226, -52,
+    0, 20, 10, 50, 51, -10, 21, 40, 1, 11, 70, 2, 90, 30, 41, 12, 60, 71, 91, 61,
+    80, 31, 13, 52, 42, 3, -20, 32, 22, 81, 100, 43, 62, 72, 101, 73, 23, 82, 33, -21,
+    92, 53, 102, 63, 110, -22, 120, 103, 83, 111, 93, -23, 121, 130, -30, 104, 112, 122, 131, 105,
+    113, 132, 123, 106, -40, 114, 124, 140, 160, 133, 150, 115, 141, 161, 151, 125, 116, 134, -41, 162,
+    126, 135, 170, 180, 152, 190, -42, 136, 200, 191, 163, 181, 220, 210, 153, -43, 240, 201, 192, 250,
+    182, 230, 154, 211, 164, 193, 221, 251, 171, 183, 241, 212, 172, 222, 142, 202, 231, 184, 242, 203,
+    173, 194, 165, 252, 155, 223, 143, 232, 213, 195, 185, 243, 174, 144, 253, 233, 204, 224, 214, 244,
+    234, 196, 166, 254, 215, 225, 145, 175, 205, 245, 235, 255, 216, 176, 146, 226, 156, 186, -51, -50,
+    256, 206, -52, 246, 236, -53,
 )
 
 
@@ -467,6 +467,13 @@
     base = [0, sizes[0] - 1, sizes[0] + sizes[1] - 2]
     each = sum(sizes) - 3
     basis_flows = sum(flow[0] == "q" for flow in flows)
+    shared_slots = max(basis_flows, len(flows) - basis_flows - blocks)
+
+    def slot_of(f, summing):
+        kind = flows[f][0]
+        if summing:
+            return f - basis_flows
+        return {"q": f, "g": shared_slots + f - basis_flows, "s": f - basis_flows - blocks}[kind]
 
     loads = [
         pltpu.make_async_copy(q_ref, q_buf, in_sem.at[0]),
@@ -493,7 +500,7 @@
 
     def push(source, target, sems, f, d, off):
         summing = sems[0] is rs_send
-        at = each * (f - summing * basis_flows) + base[d] + off - 1
+        at = each * slot_of(f, summing) + base[d] + off - 1
         kind = flows[f][0]
         if kind == "g":
             gram_at = each * (2 * (f - basis_flows) + summing) + base[d] + off - 1
@@ -513,7 +520,7 @@
             sent.append(copy)
 
     def landed(ref, sem, f, d, off):
-        at = each * (f - (sem is rs_recv) * basis_flows) + base[d] + off - 1
+        at = each * slot_of(f, sem is rs_recv) + base[d] + off - 1
         pltpu.make_async_copy(ref, ref, sem.at[at]).wait()
 
     def block(f, phase, coordinate):
@@ -799,7 +806,8 @@
         ]
     chunks = [pltpu.VMEM(sizes + ((k + 1) * width // devices, width), jnp.float32) for k in range(blocks)]
     sums_flows = sum(flow[0] != "q" for flow in flows)
-    sems = pltpu.SemaphoreType.DMA((len(flows) * (sum(sizes) - 3),))
+    slots = blocks + max(len(flows) - sums_flows, sums_flows - blocks)
+    sems = pltpu.SemaphoreType.DMA((slots * (sum(sizes) - 3),))
     sum_sems = pltpu.SemaphoreType.DMA((sums_flows * (sum(sizes) - 3),))
     scratch += chunks + chunks
     scratch += [

time: 146 us -> 146 us (level)
  no operation moved by 1% of the time
where the time goes in v6:
time: 146 us; the launch traced here: 145 us
  Pallas kernels  145 us (99%)
    pallas_call x1, Pallas kernels, right_factor(): pl.pallas_call(functools.partial(main_kernel, sizes, parts, flows, width)...  140 us
    pallas_call x1, Pallas kernels, finish(): pl.pallas_call(functools.partial(finish_kernel, 1.0 - damping, factor), o...  4.24 us

profile of v6, /device:TPU:0, one launch (start us, length us, event | category | flops | bytes accessed | tf_op | source)
XLA Modules:
  0.0 145.4 jit_solution(5140423525197487278)
XLA Ops:
  0.6 140.4 %factor_0.1 = (bf16[4,2,2,512,256]{4,3,2,1,0:T(8,128)(2,1)S(1)}, bf16[512,512]{1,0:T(8,128)(2,1)S(1)}, f32[512,256]{1,0:T(8,128)S(1)}, f32[256,4096]{1,0:T(8,128)S(1)}) custom-call(f32[256,4096]{1,0:T(8,128)} %m_ref.1, bf16[256,4096]{1,0:T(8,128)(2,1)} %g_ref.1, f32[256,512]{1,0:T(8,128)} %q_ref.1), custom_call_target="tpu_custom_call" | custom-call | tf_op jit(solution)/shard_map/factor_0/pallas_call | solution.py:838
  141.0 4.2 %finish.1 = (f32[256,4096]{1,0:T(8,128)}, bf16[256,4096]{1,0:T(8,128)(2,1)}, f32[256,512]{1,0:T(8,128)}) custom-call(bf16[16,512,256]{2,1,0:T(8,128)(2,1)S(1)} %bitcast.1, bf16[512,512]{1,0:T(8,128)(2,1)S(1)} %get-tuple-element.8.t_ref, f32[512,256]{1,0:T(8,128)S(1)} %get-tuple-element.9.q_ref, f32[256,4096]{1,0:T(8,128)S(1)} %get-tuple-element.10.m_ref), custom_call_target="tpu_custom_call" | custom-call | tf_op jit(solution)/shard_map/finish/pallas_call | solution.py:910
